TPU v7x, 128 devices: a whole 4x4x4 slice. The times are simulated.
128 devices in a mesh: dp: 8 (over z_hi, x), seq: 16 (over z_lo, y, core).
Axes of the slice: x: 4, y: 4, z: 4 (z_hi: 2, z_lo: 2; z = z_hi * 2 + z_lo), core: 2. Of those that a mesh axis runs over, the one named last changes fastest.
Arguments:
- stream: bfloat16 [8, 512, 1536], P('dp', 'seq'), may hold values from -6 to 6
- queries: bfloat16 [8, 512, 1536], P('dp', 'seq'), may hold values from -30 to 30
- new_keys: bfloat16 [8, 512, 1536], P('dp', 'seq'), may hold values from -6.5 to 6.5
- new_values: bfloat16 [8, 512, 1536], P('dp', 'seq'), may hold values from -6 to 6
- cache_keys: bfloat16 [8, 1536, 1536], P('dp', 'seq'), may hold values from -6.375 to 6.375
- cache_values: bfloat16 [8, 1536, 1536], P('dp', 'seq'), may hold values from -6 to 6
- cache_frames: int32 [8, 1536], P('dp', 'seq'), may hold values from 0 to 20, as said below
- group_index: int32 [8], P('dp'), may hold values from 4 to 7, as said below
- timestep: int32 [8], P('dp'), may hold values from 0 to 3
- gate_table: float32 [4, 1536], replicated, may hold values from 0.1 to 1.9
- attn_out_weight: bfloat16 [1536, 1536], replicated, may hold values from -0.15625 to 0.15625
- critic_in: bfloat16 [131072, 1536], P(('dp', 'seq')), may hold values from -24 to 24
- critic_cot: bfloat16 [131072, 1536], P(('dp', 'seq')), may hold values from -6 to 6
- critic_weight: bfloat16 [1536, 1536], P(('dp', 'seq')), may hold values from -0.15625 to 0.15625
Outputs:
- stream_out: bfloat16 [8, 512, 1536], P('dp', 'seq')
- critic_grad_in: bfloat16 [131072, 1536], P(('dp', 'seq'))
- critic_grad_weight: float32 [1536, 1536], P(('dp', 'seq'))
Inputs may be any that keep to these rules, and one draw needn't show every extreme that they name: `group_index`: index of the frame group; both ends are reached in every draw. `cache_frames`: sample b's cache holds the 12 frames 3 * group_index[b] - 12 to 3 * group_index[b] - 1, each in one contiguous run of slots, runs of equal length up to one slot, in a rotated order.
All inputs are finite; a program needn't handle non-finite values.
Results may differ from a plain program's by a relative error of at most 0.0045.
Values may be sent and summed in bfloat16 or wider, within the bound.
A program may use at most 128 MiB of HBM per device.

v0:
```python
import jax
import jax.numpy as jnp
from jax import lax
from jax.sharding import PartitionSpec as P

HEADS = 12
HEAD = 128
FRAMES_GROUP = 3
WINDOW_FRAMES = 9


def cut_along(array, dim, peers):
    before, after = (array.shape[:dim], array.shape[dim + 1 :])
    return jnp.moveaxis(array.reshape(*before, peers, -1, *after), dim, 0)


def summed_on_arrival(array, axis, dim):
    peers = lax.axis_size(axis)
    tiles = lax.all_to_all(cut_along(array, dim, peers), axis, 0, 0, tiled=True)
    return jnp.sum(tiles, axis=0)


def copy_for_each(array, axis):
    peers = lax.axis_size(axis)
    return lax.all_to_all(
        jnp.broadcast_to(array[None], (peers, *array.shape)), axis, 0, 0, tiled=True
    )


def of_everyone(array, axis):
    everything = copy_for_each(array, axis)
    return jnp.max(everything, axis=0)


def sent_together(arrays, axis, dim, along):
    widths = [a.shape[along] for a in arrays]
    both = jnp.concatenate(arrays, axis=along)
    out = lax.psum_scatter(both, axis, scatter_dimension=dim, tiled=True)
    return tuple(jnp.split(out, [sum(widths[:k]) for k in range(1, len(widths))], axis=along))


def critic_pass(critic_in, critic_cot, critic_weight):
    grad_in = lax.dot_general(
        critic_cot,
        lax.all_gather(critic_weight, ("dp", "seq"), axis=0, tiled=True),
        (((1,), (1,)), ((), ())),
        preferred_element_type=jnp.float32,
    ).astype(jnp.bfloat16)
    factor = float(critic_in.shape[0] * lax.axis_size(("dp", "seq"))) ** (-0.5)
    whole_term = (
        lax.dot_general(
            critic_in, critic_cot, (((0,), (0,)), ((), ())), preferred_element_type=jnp.float32
        )
        * factor
    )
    partial_rows = lax.psum_scatter(whole_term, "dp", scatter_dimension=0, tiled=True)
    grad_weight = summed_on_arrival(partial_rows, "seq", 0)
    return (grad_in, grad_weight)


def local(
    stream,
    queries,
    new_keys,
    new_values,
    cache_keys,
    cache_values,
    cache_frames,
    group_index,
    timestep,
    gate_table,
    attn_out_weight,
    critic_in,
    critic_cot,
    critic_weight,
):
    query_local = queries[0]
    own_rows = query_local.shape[0]
    width = query_local.shape[1]
    scale = HEAD ** (-0.5)
    first_frame = FRAMES_GROUP * group_index[0]
    frames = cache_frames[0]
    live_cache = (frames < first_frame) & (frames >= first_frame - WINDOW_FRAMES)
    live_local = jnp.concatenate([live_cache, jnp.ones((own_rows,), dtype=bool)])
    keys_local = jnp.concatenate([cache_keys[0], new_keys[0]], axis=0)
    values_local = jnp.concatenate([cache_values[0], new_values[0]], axis=0)
    all_queries = lax.all_gather(queries, "seq", axis=1, tiled=True)[0]
    total_rows = all_queries.shape[0]
    query_heads = all_queries.reshape(total_rows, HEADS, HEAD)
    key_heads = keys_local.reshape(-1, HEADS, HEAD)
    value_heads = values_local.reshape(-1, HEADS, HEAD)
    scores = (
        jnp.einsum("qhd,khd->hqk", query_heads, key_heads, preferred_element_type=jnp.float32)
        * scale
    )
    scores = jnp.where(live_local[None, None, :], scores, -1e30)
    local_top = jnp.max(scores, axis=2)
    global_top = of_everyone(local_top, "seq")
    weights = jnp.where(live_local[None, None, :], jnp.exp(scores - global_top[:, :, None]), 0.0)
    totals = jnp.sum(weights, axis=2)
    summed = jnp.einsum(
        "hqk,khd->qhd",
        weights.astype(jnp.bfloat16),
        value_heads,
        preferred_element_type=jnp.float32,
    )
    own_sums, own_totals = sent_together((summed.reshape(total_rows, width), totals.T), "seq", 0, 1)
    mixed = (
        (own_sums.reshape(own_rows, HEADS, HEAD) / own_totals[:, :, None])
        .reshape(own_rows, width)
        .astype(jnp.bfloat16)
    )
    projected = jnp.dot(mixed, attn_out_weight, preferred_element_type=jnp.float32)
    onehot = (
        timestep[:, None] == jnp.arange(gate_table.shape[0], dtype=jnp.int32)[None, :]
    ).astype(jnp.float32)
    gate = jnp.dot(onehot, gate_table, precision=lax.Precision.HIGHEST)
    stream_out = (stream[0].astype(jnp.float32) + gate * projected).astype(jnp.bfloat16)[None]
    grad_in, grad_weight = critic_pass(critic_in, critic_cot, critic_weight)
    return (stream_out, grad_in, grad_weight)


def solution(mesh):
    return jax.shard_map(
        local,
        mesh=mesh,
        in_specs=(
            P("dp", "seq", None),
            P("dp", "seq", None),
            P("dp", "seq", None),
            P("dp", "seq", None),
            P("dp", "seq", None),
            P("dp", "seq", None),
            P("dp", "seq"),
            P("dp"),
            P("dp"),
            P(),
            P(),
            P(("dp", "seq"), None),
            P(("dp", "seq"), None),
            P(("dp", "seq"), None),
        ),
        out_specs=(P("dp", "seq", None), P(("dp", "seq"), None), P(("dp", "seq"), None)),
        check_vma=False,
    )
```

profile of v0, /device:TPU:1, one launch (start us, length us, event | category | flops | bytes accessed | tf_op | source)
XLA Modules:
  0.0 346.9 jit_solution(15634933623455730088)
XLA Ops:
  8.0 0.0 copy-start
  8.0 0.0 all-gather.4.cloned.1.call-start
  8.1 0.7 all-gather.4.cloned.1.call-update
  8.7 0.0 all-gather.6.cloned.1.call-start
  8.8 0.7 all-gather.6.cloned.1.call-update
  9.5 0.0 reduce-scatter.5.cloned.1.call-start
  9.5 0.3 copy-done
  9.9 9.5 %convolution_multiply_fusion = f32[1536,1536]{1,0:T(8,128)} fusion(bf16[1024,1536]{1,0:T(8,128)(2,1)} %param.25, bf16[1024,1536]{1,0:T(8,128)(2,1)S(1)} %copy-done), kind=kOutput, calls=%fused_computation | convolution fusion | flops 4834197504 | bytes 15728640 | tf_op jit(solution)/shard_map/dot_general | solution.py:51
  19.4 0.0 copy-start.6
  19.4 0.0 reduce-scatter.5.cloned.1.call-update
  20.1 1.2 concatenate.26
  21.3 0.8 copy.43
  22.1 0.0 copy-start.2
  22.1 1.7 concatenate.27
  23.7 0.9 copy.44
  24.7 0.0 copy-done.6
  24.7 35.0 %all-gather.4.cloned.1.call-done = bf16[1,512,1536]{2,1,0:T(8,128)(2,1)} async-done(((bf16[1,32,1536]{2,1,0:T(8,128)(2,1)}), bf16[1,512,1536]{2,1,0:T(8,128)(2,1)}) %all-gather.4.cloned.1.call-update) | async-done | bytes 1572880 | tf_op jit(solution)/shard_map/all_gather | solution.py:87
  59.8 2.8 copy.45
  62.5 0.0 copy-done.2
  62.5 3.7 %bitcast_reduce_fusion = (f32[12,512]{1,0:T(8,128)S(1)}, f32[12,128,512]{2,1,0:T(8,128)}) fusion(pred[128]{0:T(512)(128)(4,1)S(1)} %concatenate.25, bf16[512,12,128]{0,2,1:T(8,128)(2,1)} %bitcast.47, bf16[32,12,128]{2,0,1:T(8,128)(2,1)S(1)} %copy.44, bf16[96,12,128]{2,0,1:T(8,128)(2,1)S(1)} %copy-done.2), kind=kOutput, calls=%fused_computation.4 | convolution fusion | flops 204466176 | bytes 5136512 | tf_op jit(solution)/shard_map/qhd,khd->hqk/dot_general | solution.py:93
  66.2 0.9 broadcast_in_dim.39
  67.1 4.3 %all-to-all-start = ((f32[16,12,512]{2,1,0:T(8,128)}), f32[16,12,512]{2,1,0:T(8,128)}, u32[]{:S(2)}, u32[]{:S(2)}) async-start(f32[16,12,512]{2,1,0:T(8,128)} %broadcast_in_dim.39), calls=%async_computation | async-start | bytes 1048576 | tf_op jit(solution)/shard_map/all_to_all | solution.py:25
  71.4 0.0 reduce-scatter.7.cloned.1.call-start
  71.4 1.2 copy.41
  72.6 1.8 copy.42
  74.5 7.4 %all-to-all-done = f32[16,12,512]{2,1,0:T(8,128)} async-done(((f32[16,12,512]{2,1,0:T(8,128)}), f32[16,12,512]{2,1,0:T(8,128)}, u32[]{:S(2)}, u32[]{:S(2)}) %all-to-all-start) | async-done | bytes 393248 | tf_op jit(solution)/shard_map/all_to_all | solution.py:25
  81.8 1.7 reduce_max.19
  83.5 0.0 copy-start.1
  83.5 0.0 copy-start.3
  83.5 2.9 fusion.5
  86.4 0.0 copy-done.1
  86.5 0.0 copy-done.3
  86.5 2.1 fusion.7
  88.6 2.0 pad_maximum_fusion
  90.6 4.5 %copy.51 = f32[512,1548]{1,0:T(8,128)} copy(f32[512,1548]{0,1:T(8,128)} %pad_maximum_fusion) | data formatting | bytes 6340608
  95.1 0.0 copy-start.5
  95.1 0.0 reduce-scatter.7.cloned.1.call-update
  95.8 0.1 copy-done.5
  95.8 0.2 convolution_reduce_fusion
  96.0 203.7 %all-gather.6.cloned.1.call-done = bf16[128,12,1536]{2,1,0:T(8,128)(2,1)} async-done(((bf16[1,12,1536]{2,1,0:T(8,128)(2,1)}), bf16[128,12,1536]{2,1,0:T(8,128)(2,1)}) %all-gather.6.cloned.1.call-update) | async-done | bytes 4718608 | tf_op jit(solution)/shard_map/all_gather | solution.py:45
  299.7 8.2 %reshape.51 = bf16[1536,1536]{1,0:T(8,128)(2,1)} reshape(bf16[128,12,1536]{2,1,0:T(8,128)(2,1)} %all-gather.6.cloned.1.call-done) | data formatting | bytes 9437184
  307.9 0.0 reduce-scatter.5.cloned.1.call-done
  307.9 2.5 reshape.48
  310.4 5.3 %all-to-all-start.1 = ((f32[16,12,1536]{2,1,0:T(8,128)}), f32[16,12,1536]{2,1,0:T(8,128)}, u32[]{:S(2)}, u32[]{:S(2)}) async-start(f32[16,12,1536]{2,1,0:T(8,128)} %reshape.48), calls=%async_computation.2 | async-start | bytes 3145728 | tf_op jit(solution)/shard_map/all_to_all | solution.py:19
  315.7 0.0 copy-start.4
  315.7 8.8 %convolution_convert_fusion = bf16[1024,1536]{1,0:T(8,128)(2,1)} fusion(bf16[1024,1536]{1,0:T(8,128)(2,1)S(1)} %copy-done, bf16[1536,1536]{1,0:T(8,128)(2,1)} %reshape.51), kind=kOutput, calls=%fused_computation.1 | convolution fusion | flops 4833411072 | bytes 11010048 | tf_op jit(solution)/shard_map/dot_general | solution.py:43
  324.5 0.0 reduce-scatter.7.cloned.1.call-done
  324.5 0.9 split.8
  325.5 1.2 copy.54
  326.6 0.7 split.9
  327.3 0.1 copy.55
  327.4 1.2 fusion.15
  328.6 0.0 copy-done.4
  328.6 3.9 %fusion.4 = bf16[1,32,1536]{2,1,0:T(8,128)(2,1)} fusion(bf16[32,1536]{0,1:T(8,128)(2,1)S(1)} %fusion.15, bf16[1536,1536]{1,0:T(8,128)(2,1)} %param.24, bf16[1,32,1536]{2,1,0:T(8,128)(2,1)S(1)} %copy-done.4, f32[1536]{0:T(1024)S(1)} %convolution_reduce_fusion), kind=kOutput, calls=%fused_computation.11 | convolution fusion | flops 151191552 | bytes 5019648 | tf_op jit(solution)/shard_map/dot_general | solution.py:113
  332.6 4.7 %all-to-all-done.1 = f32[16,12,1536]{2,1,0:T(8,128)} async-done(((f32[16,12,1536]{2,1,0:T(8,128)}), f32[16,12,1536]{2,1,0:T(8,128)}, u32[]{:S(2)}, u32[]{:S(2)}) %all-to-all-start.1) | async-done | bytes 1179680 | tf_op jit(solution)/shard_map/all_to_all | solution.py:19
  337.3 2.1 reduce_sum.19
  (2 shorter events, 0.0 us)
Async XLA Ops:
  8.0 1.9 copy-start
  8.0 51.7 %all-gather.4.cloned.1.call-start = ((), (), s32[]{:S(2)}) async-start(), calls=%async_computation.4 | async-start | bytes 1671168 | tf_op jit(solution)/shard_map/all_gather | solution.py:87
  8.7 291.0 %all-gather.6.cloned.1.call-start = ((), (), s32[]{:S(2)}) async-start(), calls=%async_computation.6 | async-start | bytes 6340608 | tf_op jit(solution)/shard_map/all_gather | solution.py:45
  9.5 298.4 %reduce-scatter.5.cloned.1.call-start = ((), (), s32[]{:S(2)}) async-start(), calls=%async_computation.5 | async-start | bytes 10616832 | tf_op jit(solution)/shard_map/reduce_scatter | solution.py:56
  19.4 5.2 %copy-start.6 = (s32[1,96]{1,0:T(1,128)S(1)}, s32[1,96]{1,0:T(1,128)}, u32[]{:S(2)}) copy-start(s32[1,96]{1,0:T(1,128)} %param.20) | copy-start | bytes 1156
  22.1 40.4 %copy-start.2 = (bf16[96,12,128]{2,0,1:T(8,128)(2,1)S(1)}, bf16[96,12,128]{2,0,1:T(8,128)(2,1)}, u32[]{:S(2)}) copy-start(bf16[96,12,128]{2,0,1:T(8,128)(2,1)} %copy.43) | copy-start | bytes 884740
  67.1 14.7 %all-to-all-start = ((f32[16,12,512]{2,1,0:T(8,128)}), f32[16,12,512]{2,1,0:T(8,128)}, u32[]{:S(2)}, u32[]{:S(2)}) async-start(f32[16,12,512]{2,1,0:T(8,128)} %broadcast_in_dim.39), calls=%async_computation | async-start | bytes 1048576 | tf_op jit(solution)/shard_map/all_to_all | solution.py:25
  71.4 253.1 %reduce-scatter.7.cloned.1.call-start = ((), (), s32[]{:S(2)}) async-start(), calls=%async_computation.7 | async-start | bytes 3620864
  83.5 2.9 copy-start.1
  83.5 2.9 copy-start.3
  95.1 0.7 copy-start.5
  310.4 26.9 %all-to-all-start.1 = ((f32[16,12,1536]{2,1,0:T(8,128)}), f32[16,12,1536]{2,1,0:T(8,128)}, u32[]{:S(2)}, u32[]{:S(2)}) async-start(f32[16,12,1536]{2,1,0:T(8,128)} %reshape.48), calls=%async_computation.2 | async-start | bytes 3145728 | tf_op jit(solution)/shard_map/all_to_all | solution.py:19
  315.7 12.9 %copy-start.4 = (bf16[1,32,1536]{2,1,0:T(8,128)(2,1)S(1)}, bf16[1,32,1536]{2,1,0:T(8,128)(2,1)}, u32[]{:S(2)}) copy-start(bf16[1,32,1536]{2,1,0:T(8,128)(2,1)} %param.14) | copy-start | bytes 294916
Sparse Core Ops, SparseCore 0:
  10.5 49.1 all-gather.3
  61.5 238.2 all-gather.5
Sparse Core Ops, SparseCore 1:
  19.5 133.4 reduce-scatter.4
  155.3 61.9 reduce-scatter.6
where the time goes:
time: 348 us; the launch traced here: 347 us
  waiting for transfers between devices  252 us (72%)
  local copies, waits for them, and re-layouts  29.7 us (9%)
  matrix products  28.3 us (8%)
  between operations  16.9 us (5%)
  other arithmetic  9.94 us (3%)
  starting transfers between devices  9.69 us (3%)
    all_gather x1, waiting for transfers between devices, critic_pass(): lax.all_gather(critic_weight, ('dp', 'seq'), axis=0, tiled=True)  204 us
    all_gather x1, waiting for transfers between devices, local(): all_queries = lax.all_gather(queries, 'seq', axis=1, tiled=True)[0]  35 us
    unnamed x20, local copies, waits for them, and re-layouts  17.4 us
    dot_general x1, matrix products, critic_pass(): lax.dot_general(critic_in, critic_cot, (((0,), (0,)), ((), ())), preferre...  9.53 us
    dot_general x1, matrix products, critic_pass(): lax.dot_general(critic_cot, lax.all_gather(critic_weight, ('dp', 'seq'),...  8.8 us
    all_to_all x1, waiting for transfers between devices, copy_for_each(): lax.all_to_all(jnp.broadcast_to(array[None], (peers, *array.shape)), axis...  7.38 us
  transfers between devices with their start and end apart: 6, of which 4 were waited for; matrix products, arithmetic and copies ran while one was open for 19% of the time, Pallas kernels for 0%

commit v1 on v0

v1 whole, which is shorter than its diff:
```python
import functools

import jax
import jax.numpy as jnp
from jax import lax
from jax.experimental import pallas as pl
from jax.experimental.pallas import tpu as pltpu
from jax.sharding import PartitionSpec as P

HEADS = 12
HEAD = 128
FRAMES_GROUP = 3
WINDOW_FRAMES = 9
D = 1536
HALF = 768
BF = jnp.bfloat16
F32 = jnp.float32
MESH = pl.DeviceIdType.MESH


def rem(a, n):
    return lax.rem(a, jnp.int32(n))


def div(a, n):
    return lax.div(a, jnp.int32(n))


def critic_kernel(
    cin_hbm, cot_hbm, wpad_hbm, gin_hbm, gw_ref,
    cin, cot, wown, tmp, wm, at, acc, dsend, drecv, rsend, rsend2,
    ra0, ra1, ra2, b0, b1, b2, b0s, b1s, b2s, rb0, rb1, rb2, c2, c2s, rc2, fsend, frecv, obuf,
    ld_sem, p0_s, p0_r, g1_s, g1_r, g2_s, g2_r, g3_s, g3_r, push_s, push_r,
    d_s, d_r, a_s, a_r, b_s, b_r, c_s, c_r, f_s, f_r, o_sem,
):
    dp = lax.axis_index("dp")
    seq = lax.axis_index("seq")
    zh, x = div(dp, 4), rem(dp, 4)
    zl, y, c = div(seq, 8), div(rem(seq, 8), 2), rem(seq, 2)
    z = zh * 2 + zl
    xh, xl = div(x, 2), rem(x, 2)
    plane = y * 2 + c
    partner = (dp, seq + 1 - 2 * c)

    def xdev(xx):
        return (zh * 4 + xx, seq)

    def zdev(zz):
        return (div(zz, 2) * 4 + x, rem(zz, 2) * 8 + plane)

    def ydev(yy, cc):
        return (dp, zl * 8 + yy * 2 + cc)

    def rcopy(src, dst, s_sem, r_sem, dev):
        return pltpu.make_async_remote_copy(
            src_ref=src, dst_ref=dst, send_sem=s_sem, recv_sem=r_sem, device_id=dev, device_id_type=MESH
        )

    loads = []
    for h in range(2):
        loads.append(pltpu.make_async_copy(cot_hbm.at[:, pl.ds(h * HALF, HALF)], cot.at[h], ld_sem.at[h]))
    for t in range(4):
        loads.append(pltpu.make_async_copy(cin_hbm.at[:, pl.ds(t * 384, 384)], cin.at[t], ld_sem.at[2 + t]))
    loads.append(pltpu.make_async_copy(wpad_hbm, wown, ld_sem.at[6]))
    loads[6].start()
    for ld in loads[:6]:
        ld.start()

    xs = [rem(x + s, 4) for s in (1, 2, 3)]
    ys = [rem(y + s, 4) for s in (1, 2, 3)]
    zs = [rem(z + s, 4) for s in (1, 2, 3)]
    plane_peers = [(rem(y + s, 4), c if k == 0 else 1 - c) for s in range(4) for k in range(2) if (s, k) != (0, 0)]

    barrier = pltpu.get_barrier_semaphore()
    peers = [xdev(v) for v in xs] + [zdev(v) for v in zs] + [ydev(a, b) for a, b in plane_peers]
    for dev in peers:
        pl.semaphore_signal(barrier, inc=1, device_id=dev, device_id_type=MESH)
    pl.semaphore_wait(barrier, len(peers))

    loads[6].wait()
    p0 = [
        rcopy(wown.at[b], tmp.at[plane], p0_s.at[k], p0_r.at[k], ydev(a, b))
        for k, (a, b) in enumerate(plane_peers)
    ]
    for cp in p0:
        cp.start()
    tmp[plane] = wown[c]

    def part2(ref, yy):
        return ref.at[..., pl.ds(pl.multiple_of(div(yy, 2) * 48, 48), 48), pl.ds(pl.multiple_of(512 + rem(yy, 2) * 128, 128), 128)]

    own = wm.at[c, zh, xh, xl, zl]
    g1 = []
    for k in range(3):
        g1.append(rcopy(own.at[:, pl.ds(0, 256)], own.at[:, pl.ds(0, 256)], g1_s.at[k], g1_r.at[k], xdev(xs[k])))
        g1.append(rcopy(own.at[:, pl.ds(256, 256)], own.at[:, pl.ds(256, 256)], g1_s.at[3 + k], g1_r.at[3 + k], zdev(zs[k])))
        g1.append(rcopy(part2(own, y), part2(own, y), g1_s.at[6 + k], g1_r.at[6 + k], xdev(xs[k])))
    g2 = []
    w0 = wm.at[c, zh, :, :, zl, :, pl.ds(0, 256)]
    w1 = wm.at[c, :, xh, xl, :, :, pl.ds(256, 256)]
    w2 = part2(wm.at[c, zh, :, :, zl], y)
    for k in range(3):
        g2.append(rcopy(w2, w2, g2_s.at[6 + k], g2_r.at[6 + k], zdev(zs[k])))
        g2.append(rcopy(w0, w0, g2_s.at[k], g2_r.at[k], zdev(zs[k])))
        g2.append(rcopy(w1, w1, g2_s.at[3 + k], g2_r.at[3 + k], xdev(xs[k])))
    w3 = part2(wm.at[c], y)
    g3 = [rcopy(w3, w3, g3_s.at[k], g3_r.at[k], ydev(ys[k], c)) for k in range(3)]

    for ld in loads[:6]:
        ld.wait()

    def dcopy(t):
        return rcopy(dsend.at[t], drecv.at[t], d_s.at[t], d_r.at[t], partner)

    @pl.loop(0, 4)
    def _(t):
        at[...] = cin[t].T
        dsend[t] = lax.dot_general(
            at[...], cot[1 - c], (((1,), (0,)), ((), ())), preferred_element_type=F32
        ).astype(BF)
        dcopy(t).start()
        acc[div(t, 2), rem(t, 2)] = lax.dot_general(
            at[...], cot[c], (((1,), (0,)), ((), ())), preferred_element_type=F32
        ).reshape(2, 2, 96, HALF)

        @pl.when(t == 0)
        def _():
            for cp in p0:
                cp.wait_recv()
            row = lax.broadcasted_iota(jnp.int32, (96, 128), 0)
            col = lax.broadcasted_iota(jnp.int32, (96, 128), 1)
            pick = (col == div(row, 12) * 16 + rem(row, 12)).astype(BF)
            block = jnp.dot(pick, tmp[...].reshape(128, HALF), preferred_element_type=F32).astype(BF)
            own[:, pl.ds(0, 512)] = block[:, :512]
            for yy in range(4):
                i, j = yy // 2 * 48, 512 + yy % 2 * 128

                @pl.when(y == yy)
                def _():
                    own[pl.ds(i, 48), pl.ds(j, 128)] = block[i : i + 48, j : j + 128]

            for cp in g1:
                cp.start()

        @pl.when(t == 1)
        def _():
            for cp in g1:
                cp.wait_recv()
            for cp in g2:
                cp.start()

        @pl.when(t == 2)
        def _():
            for cp in g2[0::3]:
                cp.wait_recv()
            for cp in g3:
                cp.start()

    @pl.loop(0, 4)
    def _(t):
        dcopy(t).wait_recv()
        i, j = div(t, 2), rem(t, 2)
        both = acc[i, j] + drecv[t].reshape(2, 2, 96, HALF).astype(F32)
        acc[i, j] = both
        rsend[i, j] = both[..., :512].astype(BF)
        for yy in range(4):
            rsend2[yy, i, j] = both[:, :, (yy // 2) * 48 : (yy // 2) * 48 + 48, 512 + (yy % 2) * 128 : 640 + (yy % 2) * 128].astype(BF)

    ra = []
    for k in range(3):
        ra.append(rcopy(rsend.at[div(zs[k], 2), :, :, rem(zs[k], 2), :, pl.ds(0, 256)], ra0.at[k], a_s.at[k], a_r.at[k], zdev(zs[k])))
        ra.append(rcopy(rsend.at[:, div(xs[k], 2), rem(xs[k], 2), :, :, pl.ds(256, 256)], ra1.at[k], a_s.at[3 + k], a_r.at[3 + k], xdev(xs[k])))
        ra.append(rcopy(rsend2.at[ys[k]], ra2.at[k], a_s.at[6 + k], a_r.at[6 + k], ydev(ys[k], c)))

    for cp in g2[1::3] + g2[2::3] + g3:
        cp.wait_recv()
    for cp in ra:
        cp.start()

    def pcopy(t):
        src = wm.at[c, div(t, 2), rem(t, 2)]
        return rcopy(src, src, push_s.at[t], push_r.at[t], partner)

    for t in range(4):
        pcopy(jnp.int32(t)).start()

    def ocopy(t):
        return pltpu.make_async_copy(obuf.at[t], gin_hbm.at[:, pl.ds(pl.multiple_of(t * 384, 384), 384)], o_sem.at[t])

    @pl.loop(0, 4)
    def _(t):
        pcopy(t).wait_recv()
        i, j = div(t, 2), rem(t, 2)
        dims = (((1,), (1,)), ((), ()))
        res = lax.dot_general(cot[0], wm[0, i, j].reshape(384, HALF), dims, preferred_element_type=F32)
        res = res + lax.dot_general(cot[1], wm[1, i, j].reshape(384, HALF), dims, preferred_element_type=F32)
        obuf[t] = res.astype(BF)
        ocopy(t).start()

    for cp in ra:
        cp.wait_recv()
    v0 = acc[zh, :, :, zl, :, 0:256]
    v1 = acc[:, xh, xl, :, :, 256:512]
    for k in range(3):
        v0 = v0 + ra0[k].astype(F32)
        v1 = v1 + ra1[k].astype(F32)
    b0[...] = v0
    b1[...] = v1
    b0s[...] = v0.astype(BF)
    b1s[...] = v1.astype(BF)
    v2 = rsend2[y].astype(F32)
    for k in range(3):
        v2 = v2 + ra2[k].astype(F32)
    b2[...] = v2
    b2s[...] = v2.astype(BF)

    rb = []
    for k in range(3):
        rb.append(rcopy(b2s.at[div(zs[k], 2), :, :, rem(zs[k], 2)], rb2.at[k], b_s.at[6 + k], b_r.at[6 + k], zdev(zs[k])))
        rb.append(rcopy(b0s.at[div(xs[k], 2), rem(xs[k], 2)], rb0.at[k], b_s.at[k], b_r.at[k], xdev(xs[k])))
        rb.append(rcopy(b1s.at[div(zs[k], 2), rem(zs[k], 2)], rb1.at[k], b_s.at[3 + k], b_r.at[3 + k], zdev(zs[k])))
    for cp in rb:
        cp.start()
    for cp in rb[0::3]:
        cp.wait_recv()
    v2 = b2[zh, :, :, zl]
    for k in range(3):
        v2 = v2 + rb2[k].astype(F32)
    c2[...] = v2
    c2s[...] = v2.astype(BF)
    rc = [rcopy(c2s.at[div(xs[k], 2), rem(xs[k], 2)], rc2.at[k], c_s.at[k], c_r.at[k], xdev(xs[k])) for k in range(3)]
    for cp in rc:
        cp.start()
    for cp in rb[1::3] + rb[2::3]:
        cp.wait_recv()
    r0 = b0[xh, xl]
    r1 = b1[zh, zl]
    for k in range(3):
        r0 = r0 + rb0[k].astype(F32)
        r1 = r1 + rb1[k].astype(F32)
    for cp in rc:
        cp.wait_recv()
    r2 = c2[xh, xl]
    for k in range(3):
        r2 = r2 + rc2[k].astype(F32)

    row = lax.broadcasted_iota(jnp.int32, (96, 256), 0)
    col = lax.broadcasted_iota(jnp.int32, (96, 256), 1)
    mine = (div(row, 48) == div(y, 2)) & (div(col, 128) == rem(y, 2))
    r2 = jnp.concatenate([r2, r2], axis=0)
    r2 = jnp.where(mine, jnp.concatenate([r2, r2], axis=1), 0.0)
    row = lax.broadcasted_iota(jnp.int32, (128, 96), 0)
    col = lax.broadcasted_iota(jnp.int32, (128, 96), 1)
    place = ((col == div(row, 16) * 12 + rem(row, 16)) & (rem(row, 16) < 12)).astype(BF)
    full = jnp.concatenate([r0, r1, r2], axis=1).astype(BF)
    fsend[...] = jnp.dot(place, full, preferred_element_type=F32).astype(BF).reshape(8, 16, HALF)
    fin = [
        rcopy(fsend.at[a * 2 + b], frecv.at[plane], f_s.at[k], f_r.at[k], ydev(a, b))
        for k, (a, b) in enumerate(plane_peers)
    ]
    for cp in fin:
        cp.start()
    frecv[plane] = fsend[plane]
    for cp in fin:
        cp.wait_recv()
    factor = float(131072) ** (-0.5)
    for h in range(2):
        total = frecv[h].astype(F32)
        for yy in range(1, 4):
            total = total + frecv[yy * 2 + h].astype(F32)
        gw_ref[:, pl.ds(h * HALF, HALF)] = total[:12] * factor

    for cp in p0 + g1 + g2 + g3 + ra + rb + rc + fin:
        cp.wait_send()
    for t in range(4):
        dcopy(jnp.int32(t)).wait_send()
        pcopy(jnp.int32(t)).wait_send()
        ocopy(jnp.int32(t)).wait()


def critic_pass(critic_in, critic_cot, critic_weight):
    wpad = jnp.pad(critic_weight, ((0, 4), (0, 0))).reshape(16, 2, HALF).transpose(1, 0, 2)
    dma = pltpu.SemaphoreType.DMA
    V = pltpu.VMEM
    any_spec = pl.BlockSpec(memory_space=pl.ANY)
    return pl.pallas_call(
        critic_kernel,
        out_shape=(
            jax.ShapeDtypeStruct((1024, D), BF),
            jax.ShapeDtypeStruct((12, D), F32),
        ),
        in_specs=[any_spec] * 3,
        out_specs=(any_spec, pl.BlockSpec(memory_space=pltpu.VMEM)),
        scratch_shapes=[
            V((4, 1024, 384), BF), V((2, 1024, HALF), BF), V((2, 16, HALF), BF), V((8, 16, HALF), BF),
            V((2, 2, 2, 2, 2, 96, HALF), BF), V((384, 1024), BF), V((2, 2, 2, 2, 96, HALF), F32),
            V((4, 384, HALF), BF), V((4, 384, HALF), BF),
            V((2, 2, 2, 2, 96, 512), BF), V((4, 2, 2, 2, 2, 48, 128), BF),
            V((3, 2, 2, 96, 256), BF), V((3, 2, 2, 96, 256), BF), V((3, 2, 2, 2, 2, 48, 128), BF),
            V((2, 2, 96, 256), F32), V((2, 2, 96, 256), F32), V((2, 2, 2, 2, 48, 128), F32),
            V((2, 2, 96, 256), BF), V((2, 2, 96, 256), BF), V((2, 2, 2, 2, 48, 128), BF),
            V((3, 96, 256), BF), V((3, 96, 256), BF), V((3, 2, 2, 48, 128), BF),
            V((2, 2, 48, 128), F32), V((2, 2, 48, 128), BF), V((3, 48, 128), BF),
            V((8, 16, HALF), BF), V((8, 16, HALF), BF), V((4, 1024, 384), BF),
            dma((7,)), dma((7,)), dma((7,)), dma((9,)), dma((9,)), dma((9,)), dma((9,)), dma((3,)), dma((3,)),
            dma((4,)), dma((4,)), dma((4,)), dma((4,)), dma((9,)), dma((9,)), dma((9,)), dma((9,)),
            dma((3,)), dma((3,)), dma((7,)), dma((7,)), dma((4,)),
        ],
        compiler_params=pltpu.CompilerParams(
            collective_id=0, has_side_effects=True, vmem_limit_bytes=60 * 1024 * 1024
        ),
        cost_estimate=pl.CostEstimate(flops=9663676416, bytes_accessed=20000000, transcendentals=0),
    )(critic_in, critic_cot, wpad)


def attention(stream, queries, new_keys, new_values, cache_keys, cache_values, cache_frames, group_index, timestep, gate_table, attn_out_weight):
    first_frame = FRAMES_GROUP * group_index[0]
    frames = cache_frames[0]
    live_cache = (frames < first_frame) & (frames >= first_frame - WINDOW_FRAMES)
    live = jnp.concatenate([live_cache, jnp.ones((32,), dtype=bool)]).astype(BF)
    live = jnp.broadcast_to(live[None, :], (16, HEAD))
    live = jnp.broadcast_to(live[:, None, :], (16, HEADS, HEAD))
    rows = jnp.concatenate(
        [a.reshape(-1, HEADS, HEAD) for a in (cache_keys[0], new_keys[0], cache_values[0], new_values[0], queries[0])] + [live],
        axis=0,
    ).transpose(1, 0, 2)
    rows = jnp.pad(rows, ((0, 4), (0, 0), (0, 0)))
    got = lax.all_to_all(rows, "seq", 0, 0, tiled=True)
    keys = got[:, 0:128].reshape(2048, HEAD)
    values = got[:, 128:256].reshape(2048, HEAD)
    q = got[:, 256:288].reshape(512, HEAD)
    alive = got[:, 288, :].reshape(1, 2048) > 0
    scores = lax.dot_general(q, keys, (((1,), (1,)), ((), ())), preferred_element_type=F32) * (HEAD ** (-0.5))
    scores = jnp.where(alive, scores, -1e30)
    top = jnp.max(scores, axis=1, keepdims=True)
    weights = jnp.where(alive, jnp.exp(scores - top), 0.0)
    totals = jnp.sum(weights, axis=1, keepdims=True)
    summed = jnp.dot(weights.astype(BF), values, preferred_element_type=F32)
    mixed = (summed / totals).astype(BF).reshape(16, 32, HEAD)
    back = lax.all_to_all(mixed, "seq", 0, 0, tiled=True)
    mixed = back[:HEADS].transpose(1, 0, 2).reshape(32, D)
    projected = jnp.dot(mixed, attn_out_weight, preferred_element_type=F32)
    onehot = (timestep[:, None] == jnp.arange(gate_table.shape[0], dtype=jnp.int32)[None, :]).astype(F32)
    gate = jnp.dot(onehot, gate_table, precision=lax.Precision.HIGHEST)
    return (stream[0].astype(F32) + gate * projected).astype(BF)[None]


def local(*args):
    stream_out = attention(*args[:11])
    grad_in, grad_weight = critic_pass(*args[11:])
    return (stream_out, grad_in, grad_weight)


def solution(mesh):
    three = P("dp", "seq", None)
    rows = P(("dp", "seq"), None)
    return jax.shard_map(
        local,
        mesh=mesh,
        in_specs=(three,) * 6 + (P("dp", "seq"), P("dp"), P("dp"), P(), P(), rows, rows, rows),
        out_specs=(three, rows, rows),
        check_vma=False,
    )
```

time: 348 us -> 112 us (0.32)
  waiting for transfers between devices: 252 us -> 17.2 us
  Pallas kernels: 0 us -> 62.2 us
  matrix products: 28.3 us -> 6.57 us
  local copies, waits for them, and re-layouts: 29.7 us -> 9.89 us
  between operations: 16.9 us -> 2.26 us
  other arithmetic: 9.94 us -> 1.77 us
    all_gather x2 -> x0, waiting for transfers between devices: 239 us -> none  [the longest x1 204 us: critic_pass(): lax.all_gather(critic_weight, ('dp', 'seq'), axis=0, tiled=True)]
    pallas_call x0 -> x1, Pallas kernels: none -> 62.2 us  [critic_pass(): pl.pallas_call(critic_kernel, out_shape=(jax.ShapeDtypeStruct((1024, D),...]
    dot_general x6 -> x4, matrix products: 28.3 us -> 6.57 us  [the longest x1 3.89 us: attention(): projected = jnp.dot(mixed, attn_out_weight, preferred_element_type=F32)]
    unnamed x20 -> x18, local copies, waits for them, and re-layouts: 17.4 us -> 2.71 us
    another operation x0 -> x5, local copies, waits for them, and re-layouts: none -> 5.29 us  [attention(): a.reshape(-1, HEADS, HEAD)]
    all_to_all x2, waiting for transfers between devices: 12.1 us -> 17.2 us  [the longest x1 17.2 us: attention(): got = lax.all_to_all(rows, 'seq', 0, 0, tiled=True)]
    concatenate x5 -> x1, local copies, waits for them, and re-layouts: 4.57 us -> 0.02 us  [attention(): jnp.concatenate([a.reshape(-1, HEADS, HEAD) for a in (cache_keys[0], new_...]
    reduce_sum x2 -> x1, other arithmetic: 5.05 us -> 1.1 us  [attention(): totals = jnp.sum(weights, axis=1, keepdims=True)]
  transfers between devices with their start and end apart: 6 -> 2, of which waited for: 4 -> 1; matrix products, arithmetic and copies ran while one was open for 19% -> 1% of each run, Pallas kernels for 0% -> 56%
where the time goes in v1:
time: 112 us; the launch traced here: 111 us
  Pallas kernels  62.2 us (56%)
  waiting for transfers between devices  17.2 us (15%)
  starting transfers between devices  11.4 us (10%)
  local copies, waits for them, and re-layouts  9.89 us (9%)
  matrix products  6.57 us (6%)
  between operations  2.26 us (2%)
  other arithmetic  1.77 us (2%)
    pallas_call x1, Pallas kernels, critic_pass(): pl.pallas_call(critic_kernel, out_shape=(jax.ShapeDtypeStruct((1024, D),...  62.2 us
    all_to_all x1, waiting for transfers between devices, attention(): got = lax.all_to_all(rows, 'seq', 0, 0, tiled=True)  17.2 us
    all_to_all x1, starting transfers between devices, attention(): got = lax.all_to_all(rows, 'seq', 0, 0, tiled=True)  7.33 us
    another operation x5, local copies, waits for them, and re-layouts, attention(): a.reshape(-1, HEADS, HEAD)  5.29 us
    all_to_all x1, starting transfers between devices, attention(): back = lax.all_to_all(mixed, 'seq', 0, 0, tiled=True)  4.09 us
    dot_general x1, matrix products, attention(): projected = jnp.dot(mixed, attn_out_weight, preferred_element_type=F32)  3.89 us
    unnamed x18, local copies, waits for them, and re-layouts  2.71 us
  transfers between devices with their start and end apart: 2, of which 1 were waited for; matrix products, arithmetic and copies ran while one was open for 1% of the time, Pallas kernels for 56%

profile of v1, /device:TPU:1, one launch (start us, length us, event | category | flops | bytes accessed | tf_op | source)
XLA Modules:
  0.0 111.3 jit_solution(7082940919167719336)
XLA Ops:
  0.6 0.0 copy-start
  1.3 0.7 and_bitcast_fusion
  2.0 1.2 %reshape_squeeze.16 = bf16[96,12,128]{2,1,0:T(8,128)(2,1)S(1)} reshape(bf16[1,96,1536]{2,1,0:T(8,128)(2,1)} %param.18) | data formatting | bytes 589824 | tf_op jit(solution)/shard_map/reshape;squeeze | solution.py:324
  3.2 1.0 reshape_squeeze.17
  4.2 1.2 %reshape_squeeze.18 = bf16[96,12,128]{2,1,0:T(8,128)(2,1)S(1)} reshape(bf16[1,96,1536]{2,1,0:T(8,128)(2,1)} %param.19) | data formatting | bytes 589824 | tf_op jit(solution)/shard_map/reshape;squeeze | solution.py:324
  5.3 1.0 reshape_squeeze.19
  6.3 1.0 reshape_squeeze.20
  7.3 0.0 copy-start.4
  7.4 0.1 constant_dynamic-update-slice_fusion.2
  7.5 0.2 copy.30
  7.7 1.1 %pad.9.clone = bf16[16,304,128]{2,1,0:T(8,128)(2,1)} pad(bf16[12,304,128]{2,1,0:T(8,128)(2,1)S(1)} %copy.30, bf16[]{:T(256)} %constant.5.clone.1), padding=0_4x0_0x0_0 | pad | bytes 2179074 | tf_op jit(solution)/shard_map/jit(_pad)/pad | solution.py:327
  8.9 7.3 %all-to-all-start = ((bf16[16,304,128]{2,1,0:T(8,128)(2,1)}), bf16[16,304,128]{2,1,0:T(8,128)(2,1)S(1)}, u32[]{:S(2)}, u32[]{:S(2)}) async-start(bf16[16,304,128]{2,1,0:T(8,128)(2,1)} %pad.9.clone), calls=%async_computation | async-start | bytes 2490368 | tf_op jit(solution)/shard_map/all_to_all | solution.py:328
  16.2 0.0 copy-done.4
  16.2 0.6 copy.39
  16.9 17.2 %all-to-all-done = bf16[16,304,128]{2,1,0:T(8,128)(2,1)S(1)} async-done(((bf16[16,304,128]{2,1,0:T(8,128)(2,1)}), bf16[16,304,128]{2,1,0:T(8,128)(2,1)S(1)}, u32[]{:S(2)}, u32[]{:S(2)}) %all-to-all-start) | async-done | bytes 1245216 | tf_op jit(solution)/shard_map/all_to_all | solution.py:328
  34.1 0.1 fusion.24
  34.2 0.9 fusion
  35.0 1.1 fusion.1
  36.1 1.7 %fusion.12 = bf16[512,128]{1,0:T(8,128)(2,1)} fusion(bf16[2048,128]{1,0:T(8,128)(2,1)S(1)} %bitcast.43, f32[512,2048]{1,0:T(8,128)S(1)} %get-tuple-element.10, f32[512]{0:T(512)S(1)} %get-tuple-element.9, pred[2048]{0:T(1024)(128)(4,1)S(1)} %compare_bitcast_fusion, f32[512]{0:T(512)S(1)} %fusion.1), kind=kOutput, calls=%fused_computation.13 | convolution fusion | flops 273809408 | bytes 4855808 | tf_op jit(solution)/shard_map/dot_general | solution.py:338
  37.8 4.1 %all-to-all-start.1 = ((bf16[16,32,128]{2,1,0:T(8,128)(2,1)}), bf16[16,32,128]{2,1,0:T(8,128)(2,1)S(1)}, u32[]{:S(2)}, u32[]{:S(2)}) async-start(bf16[16,32,128]{2,1,0:T(8,128)(2,1)} %bitcast.10), calls=%async_computation.1 | async-start | bytes 262144 | tf_op jit(solution)/shard_map/all_to_all | solution.py:340
  41.9 0.0 copy-start.3
  41.9 62.2 %shard_map.157 = (bf16[1024,1536]{1,0:T(8,128)(2,1)}, f32[12,1536]{1,0:T(8,128)}) custom-call(bf16[1024,1536]{1,0:T(8,128)(2,1)} %cin_hbm.1, bf16[1024,1536]{1,0:T(8,128)(2,1)} %cot_hbm.1, bf16[2,16,768]{2,1,0:T(8,128)(2,1)} %bitcast.45), custom_call_target="tpu_custom_call" | custom-call | flops 9663676416 | bytes 20000000 | tf_op jit(solution)/shard_map/pallas_call | solution.py:286
  104.1 0.0 copy-start.1
  104.9 0.0 copy-done
  104.9 0.2 convolution_reduce_fusion
  105.1 0.0 all-to-all-done.1
  105.1 0.0 copy-done.3
  105.1 3.9 %fusion.5 = bf16[1,32,1536]{2,1,0:T(8,128)(2,1)} fusion(bf16[1536,1536]{1,0:T(8,128)(2,1)} %param.24, bf16[1,32,1536]{2,1,0:T(8,128)(2,1)S(1)} %copy-done.3, f32[1536]{0:T(1024)S(1)} %convolution_reduce_fusion, bf16[16,32,128]{2,1,0:T(8,128)(2,1)S(1)} %all-to-all-done.1), kind=kOutput, calls=%fused_computation.8 | convolution fusion | flops 151191552 | bytes 5021696 | tf_op jit(solution)/shard_map/dot_general | solution.py:342
  109.0 0.0 copy-done.1
  109.0 0.0 copy-start.2
  109.0 1.7 %copy.49 = bf16[1024,1536]{1,0:T(8,128)(2,1)} copy(bf16[1024,1536]{1,0:T(8,128)(2,1)S(1)} %copy-done.1) | data formatting | bytes 6291456
  110.7 0.0 copy-done.2
  110.7 0.6 copy.50
  (10 shorter events, 0.2 us)
Async XLA Ops:
  0.6 104.3 %copy-start = (f32[4,1536]{1,0:T(4,128)S(1)}, f32[4,1536]{1,0:T(4,128)}, u32[]{:S(2)}) copy-start(f32[4,1536]{1,0:T(4,128)} %param.23) | copy-start | bytes 73732
  7.3 8.9 %copy-start.4 = (bf16[12,1536]{1,0:T(8,128)(2,1)S(1)}, bf16[12,1536]{1,0:T(8,128)(2,1)}, u32[]{:S(2)}) copy-start(bf16[12,1536]{1,0:T(8,128)(2,1)} %param.27) | copy-start | bytes 110596
  8.9 25.2 %all-to-all-start = ((bf16[16,304,128]{2,1,0:T(8,128)(2,1)}), bf16[16,304,128]{2,1,0:T(8,128)(2,1)S(1)}, u32[]{:S(2)}, u32[]{:S(2)}) async-start(bf16[16,304,128]{2,1,0:T(8,128)(2,1)} %pad.9.clone), calls=%async_computation | async-start | bytes 2490368 | tf_op jit(solution)/shard_map/all_to_all | solution.py:328
  37.8 67.3 %all-to-all-start.1 = ((bf16[16,32,128]{2,1,0:T(8,128)(2,1)}), bf16[16,32,128]{2,1,0:T(8,128)(2,1)S(1)}, u32[]{:S(2)}, u32[]{:S(2)}) async-start(bf16[16,32,128]{2,1,0:T(8,128)(2,1)} %bitcast.10), calls=%async_computation.1 | async-start | bytes 262144 | tf_op jit(solution)/shard_map/all_to_all | solution.py:340
  41.9 63.2 %copy-start.3 = (bf16[1,32,1536]{2,1,0:T(8,128)(2,1)S(1)}, bf16[1,32,1536]{2,1,0:T(8,128)(2,1)}, u32[]{:S(2)}) copy-start(bf16[1,32,1536]{2,1,0:T(8,128)(2,1)} %param.14) | copy-start | bytes 294916
  104.1 4.9 %copy-start.1 = (bf16[1024,1536]{1,0:T(8,128)(2,1)S(1)}, bf16[1024,1536]{1,0:T(8,128)(2,1)}, u32[]{:S(2)}) copy-start(bf16[1024,1536]{1,0:T(8,128)(2,1)} %get-tuple-element.15) | copy-start | bytes 9437188
  109.0 1.7 %copy-start.2 = (f32[12,1536]{1,0:T(8,128)S(1)}, f32[12,1536]{1,0:T(8,128)}, u32[]{:S(2)}) copy-start(f32[12,1536]{1,0:T(8,128)} %get-tuple-element.16) | copy-start | bytes 221188

commit v2 on v1

v2 whole, which is shorter than its diff:
```python
import functools

import jax
import jax.numpy as jnp
from jax import lax
from jax.experimental import pallas as pl
from jax.experimental.pallas import tpu as pltpu
from jax.sharding import PartitionSpec as P

HEADS = 12
HEAD = 128
FRAMES_GROUP = 3
WINDOW_FRAMES = 9
D = 1536
HALF = 768
BF = jnp.bfloat16
F32 = jnp.float32
MESH = pl.DeviceIdType.MESH


def rem(a, n):
    return lax.rem(a, jnp.int32(n))


def div(a, n):
    return lax.div(a, jnp.int32(n))


SCOPE = [None]


def sc(name=None):
    if SCOPE[0] is not None:
        SCOPE[0].__exit__(None, None, None)
    SCOPE[0] = None
    if name and PROFILE:
        SCOPE[0] = jax.named_scope(name)
        SCOPE[0].__enter__()


PROFILE = False


def owner(h):
    u, r = h // 3, h % 3
    zl = u // 2
    y = (u % 2) * 2 + (zl if r < 2 else 1 - zl)
    return zl * 8 + y * 2 + (r if r < 2 else 1)


def fused_kernel(
    stream_ref, q_hbm, nk_hbm, nv_hbm, ck_hbm, cv_hbm, frames_ref, group_ref, step_ref, gate_ref, aow_hbm,
    cin_hbm, cot_hbm, w_ref, so_ref, gin_hbm, gw_ref,
    kbuf, vbuf, qbuf, aow, msg, got, ob, mixed,
    cin, cot, wown, tmp, wm, at, acc, dsend, drecv, rsend, rsend2,
    ra0, ra1, ra2, b0, b1, b2, b0s, b1s, b2s, rb0, rb1, rb2, c2, c2s, rc2, fsend, frecv, obuf,
    ld_sem, p0_s, p0_r, g1_s, g1_r, g2_s, g2_r, g3_s, g3_r, push_s, push_r,
    d_s, d_r, a_s, a_r, b_s, b_r, c_s, c_r, f_s, f_r, o_sem, m_s, m_r, o_s, o_r,
):
    dp = lax.axis_index("dp")
    seq = lax.axis_index("seq")
    zh, x = div(dp, 4), rem(dp, 4)
    zl, y, c = div(seq, 8), div(rem(seq, 8), 2), rem(seq, 2)
    z = zh * 2 + zl
    xh, xl = div(x, 2), rem(x, 2)
    plane = y * 2 + c
    partner = (dp, seq + 1 - 2 * c)

    def xdev(xx):
        return (zh * 4 + xx, seq)

    def zdev(zz):
        return (div(zz, 2) * 4 + x, rem(zz, 2) * 8 + plane)

    def ydev(yy, cc):
        return (dp, zl * 8 + yy * 2 + cc)

    def rcopy(src, dst, s_sem, r_sem, dev):
        return pltpu.make_async_remote_copy(
            src_ref=src, dst_ref=dst, send_sem=s_sem, recv_sem=r_sem, device_id=dev, device_id_type=MESH
        )

    pairs = [(q_hbm, qbuf), (ck_hbm, kbuf.at[pl.ds(0, 96)]), (nk_hbm, kbuf.at[pl.ds(96, 32)]),
             (cv_hbm, vbuf.at[pl.ds(0, 96)]), (nv_hbm, vbuf.at[pl.ds(96, 32)])]
    pairs += [(cot_hbm.at[:, pl.ds(h * HALF, HALF)], cot.at[h]) for h in range(2)]
    pairs += [(cin_hbm.at[:, pl.ds(t * 384, 384)], cin.at[t]) for t in range(4)]
    pairs += [(aow_hbm, aow)]
    loads = [pltpu.make_async_copy(a, b, ld_sem.at[k]) for k, (a, b) in enumerate(pairs)]
    for ld in loads:
        ld.start()

    xs = [rem(x + s, 4) for s in (1, 2, 3)]
    ys = [rem(y + s, 4) for s in (1, 2, 3)]
    zs = [rem(z + s, 4) for s in (1, 2, 3)]
    plane_peers = [(rem(y + s, 4), c if k == 0 else 1 - c) for s in range(4) for k in range(2) if (s, k) != (0, 0)]
    others = [rem(seq + s, 16) for s in range(1, 16)]

    sc("barrier")
    barrier = pltpu.get_barrier_semaphore()
    peers = [xdev(v) for v in xs] + [((1 - zh) * 4 + x, v * 8 + plane) for v in range(2)] + [(dp, v) for v in others]
    for dev in peers:
        pl.semaphore_signal(barrier, inc=1, device_id=dev, device_id_type=MESH)
    for h in range(2):
        wown[h] = jnp.zeros((16, HALF), BF)
        wown[h, pl.ds(0, 12), :] = w_ref[:, pl.ds(h * HALF, HALF)]
    pl.semaphore_wait(barrier, len(peers))

    p0 = [
        rcopy(wown.at[b], tmp.at[plane], p0_s.at[k], p0_r.at[k], ydev(a, b))
        for k, (a, b) in enumerate(plane_peers)
    ]
    for cp in p0:
        cp.start()
    tmp[plane] = wown[c]

    sc("msg")
    for ld in loads[:5]:
        ld.wait()
    first = FRAMES_GROUP * group_ref[0]
    frames = frames_ref[...]
    live = jnp.where((frames < first) & (frames >= first - WINDOW_FRAMES), 1.0, 0.0)
    live = jnp.broadcast_to(live, (16, 96)).astype(BF)
    for h in range(HEADS):
        cols = pl.ds(h * HEAD, HEAD)
        msg[h, pl.ds(0, 128), :] = kbuf[:, cols]
        msg[h, pl.ds(128, 128), :] = vbuf[:, cols]
        msg[h, pl.ds(256, 32), :] = qbuf[:, cols]
        msg[h, pl.ds(288, 16), :] = jnp.ones((16, HEAD), BF)
        msg[h, pl.ds(288, 16), pl.ds(0, 96)] = live

    def mcopy(h):
        return rcopy(msg.at[h], got.at[seq], m_s.at[h], m_r.at[seq], (dp, owner(h)))

    def part2(ref, yy):
        return ref.at[..., pl.ds(pl.multiple_of(div(yy, 2) * 48, 48), 48), pl.ds(pl.multiple_of(512 + rem(yy, 2) * 128, 128), 128)]

    own = wm.at[c, zh, xh, xl, zl]
    g1 = []
    for k in range(3):
        g1.append(rcopy(own.at[:, pl.ds(0, 256)], own.at[:, pl.ds(0, 256)], g1_s.at[k], g1_r.at[k], xdev(xs[k])))
        g1.append(rcopy(own.at[:, pl.ds(256, 256)], own.at[:, pl.ds(256, 256)], g1_s.at[3 + k], g1_r.at[3 + k], zdev(zs[k])))
        g1.append(rcopy(part2(own, y), part2(own, y), g1_s.at[6 + k], g1_r.at[6 + k], xdev(xs[k])))
    g2 = []
    w0 = wm.at[c, zh, :, :, zl, :, pl.ds(0, 256)]
    w1 = wm.at[c, :, xh, xl, :, :, pl.ds(256, 256)]
    w2 = part2(wm.at[c, zh, :, :, zl], y)
    for k in range(3):
        g2.append(rcopy(w2, w2, g2_s.at[6 + k], g2_r.at[6 + k], zdev(zs[k])))
        g2.append(rcopy(w0, w0, g2_s.at[k], g2_r.at[k], zdev(zs[k])))
        g2.append(rcopy(w1, w1, g2_s.at[3 + k], g2_r.at[3 + k], xdev(xs[k])))
    w3 = part2(wm.at[c], y)
    g3 = [rcopy(w3, w3, g3_s.at[k], g3_r.at[k], ydev(ys[k], c)) for k in range(3)]

    sc("ldwait")
    for ld in loads[5:11]:
        ld.wait()
    sc()

    def dcopy(t):
        return rcopy(dsend.at[t], drecv.at[t], d_s.at[t], d_r.at[t], partner)

    @pl.loop(0, 4)
    def _(t):
        sc("gw")
        at[...] = cin[t].T
        dsend[t] = lax.dot_general(
            at[...], cot[1 - c], (((1,), (0,)), ((), ())), preferred_element_type=F32
        ).astype(BF)
        dcopy(t).start()
        acc[div(t, 2), rem(t, 2)] = lax.dot_general(
            at[...], cot[c], (((1,), (0,)), ((), ())), preferred_element_type=F32
        ).reshape(2, 2, 96, HALF)
        sc("comm0")

        @pl.when(t == 0)
        def _():
            for cp in p0:
                cp.wait_recv()
            row = lax.broadcasted_iota(jnp.int32, (96, 128), 0)
            col = lax.broadcasted_iota(jnp.int32, (96, 128), 1)
            pick = (col == div(row, 12) * 16 + rem(row, 12)).astype(BF)
            block = jnp.dot(pick, tmp[...].reshape(128, HALF), preferred_element_type=F32).astype(BF)
            own[:, pl.ds(0, 512)] = block[:, :512]
            for yy in range(4):
                i, j = yy // 2 * 48, 512 + yy % 2 * 128

                @pl.when(y == yy)
                def _():
                    own[pl.ds(i, 48), pl.ds(j, 128)] = block[i : i + 48, j : j + 128]

            for cp in g1:
                cp.start()

        sc("comm1")

        @pl.when(t == 1)
        def _():
            for cp in g1:
                cp.wait_recv()
            for cp in g2:
                cp.start()
            for h in range(HEADS):

                @pl.when(seq != owner(h))
                def _():
                    mcopy(h).start()

                @pl.when(seq == owner(h))
                def _():
                    got[seq] = msg[h]

        sc()

    @pl.loop(0, 4)
    def _(t):
        sc("dwait")
        dcopy(t).wait_recv()
        sc("chipsum")
        i, j = div(t, 2), rem(t, 2)
        both = acc[i, j] + drecv[t].reshape(2, 2, 96, HALF).astype(F32)
        acc[i, j] = both
        rsend[i, j] = both[..., :512].astype(BF)
        for yy in range(4):
            rsend2[yy, i, j] = both[:, :, (yy // 2) * 48 : (yy // 2) * 48 + 48, 512 + (yy % 2) * 128 : 640 + (yy % 2) * 128].astype(BF)
        sc()

    sc("rastart")
    ra = []
    for k in range(3):
        ra.append(rcopy(rsend.at[div(zs[k], 2), :, :, rem(zs[k], 2), :, pl.ds(0, 256)], ra0.at[k], a_s.at[k], a_r.at[k], zdev(zs[k])))
        ra.append(rcopy(rsend.at[:, div(xs[k], 2), rem(xs[k], 2), :, :, pl.ds(256, 256)], ra1.at[k], a_s.at[3 + k], a_r.at[3 + k], xdev(xs[k])))
        ra.append(rcopy(rsend2.at[ys[k]], ra2.at[k], a_s.at[6 + k], a_r.at[6 + k], ydev(ys[k], c)))
    for cp in ra:
        cp.start()

    sc("g2wait")
    for cp in g2[0::3]:
        cp.wait_recv()
    for cp in g3:
        cp.start()
    sc("g2wait2")
    for cp in g2[1::3] + g2[2::3]:
        cp.wait_recv()

    def pcopy(k, t):
        src = wm.at[c, div(t, 2), rem(t, 2), :, :, :, pl.ds(512 * k, 512 - 256 * k)]
        return rcopy(src, src, push_s.at[4 * k + t], push_r.at[4 * k + t], partner)

    for t in range(4):
        pcopy(0, jnp.int32(t)).start()

    double = rem(y, 2) == zl
    active = double | (c == 1)
    head = 3 * (zl * 2 + div(y, 2)) + jnp.where(double, c, 2)

    def mixcopy(k):
        return rcopy(ob.at[others[k]], mixed.at[head], o_s.at[k], o_r.at[head], (dp, others[k]))

    sc("attwait")

    @pl.when(active)
    def _():
        for src in others:
            rcopy(msg.at[0], got.at[src], m_s.at[0], m_r.at[src], partner).wait_recv()

    sc("att")

    @pl.when(active)
    def _():
        alive = jnp.concatenate([got[j, pl.ds(288, 16), :] for j in range(16)], axis=1)[0:1].astype(F32) > 0.5

        @pl.loop(0, 4)
        def _(i):
            q = got[pl.ds(i * 4, 4), pl.ds(256, 32), :].reshape(128, HEAD)
            keys = got[:, pl.ds(0, 128), :].reshape(2048, HEAD)
            values = got[:, pl.ds(128, 128), :].reshape(2048, HEAD)
            scores = lax.dot_general(q, keys, (((1,), (1,)), ((), ())), preferred_element_type=F32) * (HEAD ** (-0.5))
            scores = jnp.where(alive, scores, -1e30)
            top = jnp.max(scores, axis=1, keepdims=True)
            weights = jnp.where(alive, jnp.exp(scores - top), 0.0)
            totals = jnp.sum(weights, axis=1, keepdims=True)
            summed = jnp.dot(weights.astype(BF), values, preferred_element_type=F32)
            ob[pl.ds(i * 4, 4)] = (summed / totals).astype(BF).reshape(4, 32, HEAD)

        for k in range(15):
            mixcopy(k).start()
        mixed[head] = ob[seq]

    sc("g3wait")
    for cp in g3:
        cp.wait_recv()
    for t in range(4):
        pcopy(1, jnp.int32(t)).start()
    sc()

    def ocopy(t):
        return pltpu.make_async_copy(obuf.at[t], gin_hbm.at[:, pl.ds(pl.multiple_of(t * 384, 384), 384)], o_sem.at[t])

    rb = []
    for k in range(3):
        rb.append(rcopy(b2s.at[div(zs[k], 2), :, :, rem(zs[k], 2)], rb2.at[k], b_s.at[6 + k], b_r.at[6 + k], zdev(zs[k])))
        rb.append(rcopy(b0s.at[div(xs[k], 2), rem(xs[k], 2)], rb0.at[k], b_s.at[k], b_r.at[k], xdev(xs[k])))
        rb.append(rcopy(b1s.at[div(zs[k], 2), rem(zs[k], 2)], rb1.at[k], b_s.at[3 + k], b_r.at[3 + k], zdev(zs[k])))
    rc = [rcopy(c2s.at[div(xs[k], 2), rem(xs[k], 2)], rc2.at[k], c_s.at[k], c_r.at[k], xdev(xs[k])) for k in range(3)]

    @pl.loop(0, 4)
    def _(t):
        sc("pwait")
        pcopy(0, t).wait_recv()
        pcopy(1, t).wait_recv()
        sc("gin")
        i, j = div(t, 2), rem(t, 2)
        dims = (((1,), (1,)), ((), ()))
        res = lax.dot_general(cot[0], wm[0, i, j].reshape(384, HALF), dims, preferred_element_type=F32)
        res = res + lax.dot_general(cot[1], wm[1, i, j].reshape(384, HALF), dims, preferred_element_type=F32)
        obuf[t] = res.astype(BF)
        ocopy(t).start()

        sc("rawait")

        @pl.when(t == 0)
        def _():
            for cp in ra:
                cp.wait_recv()
            v0 = acc[zh, :, :, zl, :, 0:256]
            v1 = acc[:, xh, xl, :, :, 256:512]
            for k in range(3):
                v0 = v0 + ra0[k].astype(F32)
                v1 = v1 + ra1[k].astype(F32)
            b0[...] = v0
            b1[...] = v1
            b0s[...] = v0.astype(BF)
            b1s[...] = v1.astype(BF)
            v2 = rsend2[y].astype(F32)
            for k in range(3):
                v2 = v2 + ra2[k].astype(F32)
            b2[...] = v2
            b2s[...] = v2.astype(BF)
            for cp in rb:
                cp.start()

        sc("rbwait")

        @pl.when(t == 2)
        def _():
            for cp in rb[0::3]:
                cp.wait_recv()
            v2 = b2[zh, :, :, zl]
            for k in range(3):
                v2 = v2 + rb2[k].astype(F32)
            c2[...] = v2
            c2s[...] = v2.astype(BF)
            for cp in rc:
                cp.start()

        sc()

    sc("rbwait2")
    for cp in rb[1::3] + rb[2::3]:
        cp.wait_recv()
    r0 = b0[xh, xl]
    r1 = b1[zh, zl]
    for k in range(3):
        r0 = r0 + rb0[k].astype(F32)
        r1 = r1 + rb1[k].astype(F32)
    sc("rcwait")
    for cp in rc:
        cp.wait_recv()
    sc("last")
    r2 = c2[xh, xl]
    for k in range(3):
        r2 = r2 + rc2[k].astype(F32)

    row = lax.broadcasted_iota(jnp.int32, (96, 256), 0)
    col = lax.broadcasted_iota(jnp.int32, (96, 256), 1)
    mine = (div(row, 48) == div(y, 2)) & (div(col, 128) == rem(y, 2))
    r2 = jnp.concatenate([r2, r2], axis=0)
    r2 = jnp.where(mine, jnp.concatenate([r2, r2], axis=1), 0.0)
    row = lax.broadcasted_iota(jnp.int32, (128, 96), 0)
    col = lax.broadcasted_iota(jnp.int32, (128, 96), 1)
    place = ((col == div(row, 16) * 12 + rem(row, 16)) & (rem(row, 16) < 12)).astype(BF)
    full = jnp.concatenate([r0, r1, r2], axis=1).astype(BF)
    fsend[...] = jnp.dot(place, full, preferred_element_type=F32).astype(BF).reshape(8, 16, HALF)
    fin = [
        rcopy(fsend.at[a * 2 + b], frecv.at[plane], f_s.at[k], f_r.at[k], ydev(a, b))
        for k, (a, b) in enumerate(plane_peers)
    ]
    for cp in fin:
        cp.start()
    frecv[plane] = fsend[plane]

    sc("mixwait")
    for h in range(HEADS):

        @pl.when(seq != owner(h))
        def _():
            rcopy(ob.at[0], mixed.at[h], o_s.at[0], o_r.at[h], partner).wait_recv()

    loads[11].wait()
    sc("proj")
    joined = jnp.concatenate([mixed[h] for h in range(HEADS)], axis=1)
    projected = jnp.dot(joined, aow[...], preferred_element_type=F32)
    row = lax.broadcasted_iota(jnp.int32, (4, D), 0)
    gate = jnp.sum(jnp.where(row == step_ref[0], gate_ref[...], 0.0), axis=0, keepdims=True)
    so_ref[...] = (stream_ref[...].astype(F32) + gate * projected).astype(BF)

    sc("finwait")
    for cp in fin:
        cp.wait_recv()
    sc("drain")
    factor = float(131072) ** (-0.5)
    for h in range(2):
        total = frecv[h].astype(F32)
        for yy in range(1, 4):
            total = total + frecv[yy * 2 + h].astype(F32)
        gw_ref[:, pl.ds(h * HALF, HALF)] = total[:12] * factor

    for cp in p0 + g1 + g2 + g3 + ra + rb + rc + fin:
        cp.wait_send()
    for t in range(4):
        dcopy(jnp.int32(t)).wait_send()
        pcopy(0, jnp.int32(t)).wait_send()
        pcopy(1, jnp.int32(t)).wait_send()
        ocopy(jnp.int32(t)).wait()
    for h in range(HEADS):

        @pl.when(seq != owner(h))
        def _():
            mcopy(h).wait_send()

    @pl.when(active)
    def _():
        for k in range(15):
            mixcopy(k).wait_send()

    sc()


def local(stream, queries, new_keys, new_values, cache_keys, cache_values, cache_frames, group_index, timestep, gate_table, attn_out_weight, critic_in, critic_cot, critic_weight):
    dma = pltpu.SemaphoreType.DMA
    V = pltpu.VMEM
    anywhere = pl.BlockSpec(memory_space=pl.ANY)
    vmem = pl.BlockSpec(memory_space=pltpu.VMEM)
    smem = pl.BlockSpec(memory_space=pltpu.SMEM)
    so, gin, gw = pl.pallas_call(
        fused_kernel,
        out_shape=(
            jax.ShapeDtypeStruct((32, D), BF),
            jax.ShapeDtypeStruct((1024, D), BF),
            jax.ShapeDtypeStruct((12, D), F32),
        ),
        in_specs=[vmem] + [anywhere] * 5 + [vmem, smem, smem, vmem] + [anywhere] * 3 + [vmem],
        out_specs=(vmem, anywhere, vmem),
        scratch_shapes=[
            V((128, D), BF), V((128, D), BF), V((32, D), BF), V((D, D), BF), V((HEADS, 304, HEAD), BF),
            V((16, 304, HEAD), BF), V((16, 32, HEAD), BF), V((HEADS, 32, HEAD), BF),
            V((4, 1024, 384), BF), V((2, 1024, HALF), BF), V((2, 16, HALF), BF), V((8, 16, HALF), BF),
            V((2, 2, 2, 2, 2, 96, HALF), BF), V((384, 1024), BF), V((2, 2, 2, 2, 96, HALF), F32),
            V((4, 384, HALF), BF), V((4, 384, HALF), BF),
            V((2, 2, 2, 2, 96, 512), BF), V((4, 2, 2, 2, 2, 48, 128), BF),
            V((3, 2, 2, 96, 256), BF), V((3, 2, 2, 96, 256), BF), V((3, 2, 2, 2, 2, 48, 128), BF),
            V((2, 2, 96, 256), F32), V((2, 2, 96, 256), F32), V((2, 2, 2, 2, 48, 128), F32),
            V((2, 2, 96, 256), BF), V((2, 2, 96, 256), BF), V((2, 2, 2, 2, 48, 128), BF),
            V((3, 96, 256), BF), V((3, 96, 256), BF), V((3, 2, 2, 48, 128), BF),
            V((2, 2, 48, 128), F32), V((2, 2, 48, 128), BF), V((3, 48, 128), BF),
            V((8, 16, HALF), BF), V((8, 16, HALF), BF), V((4, 1024, 384), BF),
            dma((12,)), dma((7,)), dma((7,)), dma((9,)), dma((9,)), dma((9,)), dma((9,)), dma((3,)), dma((3,)),
            dma((8,)), dma((8,)), dma((4,)), dma((4,)), dma((9,)), dma((9,)), dma((9,)), dma((9,)),
            dma((3,)), dma((3,)), dma((7,)), dma((7,)), dma((4,)), dma((12,)), dma((16,)), dma((15,)), dma((12,)),
        ],
        compiler_params=pltpu.CompilerParams(
            collective_id=0, has_side_effects=True, vmem_limit_bytes=60 * 1024 * 1024
        ),
        cost_estimate=pl.CostEstimate(flops=10500000000, bytes_accessed=25000000, transcendentals=1000000),
    )(
        stream[0], queries[0], new_keys[0], new_values[0], cache_keys[0], cache_values[0], cache_frames,
        group_index, timestep, gate_table, attn_out_weight, critic_in, critic_cot, critic_weight,
    )
    return (so[None], gin, gw)


def solution(mesh):
    three = P("dp", "seq", None)
    rows = P(("dp", "seq"), None)
    return jax.shard_map(
        local,
        mesh=mesh,
        in_specs=(three,) * 6 + (P("dp", "seq"), P("dp"), P("dp"), P(), P(), rows, rows, rows),
        out_specs=(three, rows, rows),
        check_vma=False,
    )
```

time: 112 us -> 79 us (0.71)
  waiting for transfers between devices: 17.2 us -> 0 us
  starting transfers between devices: 11.4 us -> 0 us
  Pallas kernels: 62.2 us -> 70.9 us
  matrix products: 6.57 us -> 0 us
  local copies, waits for them, and re-layouts: 9.89 us -> 5.97 us
  other arithmetic: 1.77 us -> 0 us
    all_to_all x2 -> x0, waiting for transfers between devices: 17.2 us -> none  [the longest x1 17.2 us: attention(): got = lax.all_to_all(rows, 'seq', 0, 0, tiled=True)]
    all_to_all x2 -> x0, starting transfers between devices: 11.4 us -> none  [the longest x1 7.33 us: attention(): got = lax.all_to_all(rows, 'seq', 0, 0, tiled=True)]
    pallas_call x1, Pallas kernels: 62.2 us -> 70.9 us  [local(): pl.pallas_call(fused_kernel, out_shape=(jax.ShapeDtypeStruct((32, D), BF)...]
    dot_general x4 -> x0, matrix products: 6.57 us -> none  [the longest x1 3.89 us: attention(): projected = jnp.dot(mixed, attn_out_weight, preferred_element_type=F32)]
    another operation x5 -> x0, local copies, waits for them, and re-layouts: 5.29 us -> none  [attention(): a.reshape(-1, HEADS, HEAD)]
    unnamed x18 -> x5, local copies, waits for them, and re-layouts: 2.71 us -> 5.97 us
    pad x2 -> x0, local copies, waits for them, and re-layouts: 1.15 us -> none  [the longest x1 1.14 us: attention(): rows = jnp.pad(rows, ((0, 4), (0, 0), (0, 0)))]
  transfers between devices with their start and end apart: 2 -> 0, of which waited for: 1 -> 0; matrix products, arithmetic and copies ran while one was open for 1% -> 0% of each run, Pallas kernels for 56% -> 0%
where the time goes in v2:
time: 79 us; the launch traced here: 78.8 us
  Pallas kernels  70.9 us (90%)
  local copies, waits for them, and re-layouts  5.97 us (8%)
  between operations  1.94 us (2%)
    pallas_call x1, Pallas kernels, local(): pl.pallas_call(fused_kernel, out_shape=(jax.ShapeDtypeStruct((32, D), BF)...  70.9 us
    unnamed x5, local copies, waits for them, and re-layouts  5.97 us

profile of v2, /device:TPU:1, one launch (start us, length us, event | category | flops | bytes accessed | tf_op | source)
XLA Modules:
  0.0 78.8 jit_solution(10019582584715275179)
XLA Ops:
  1.9 70.9 %shard_map.157 = (bf16[32,1536]{1,0:T(8,128)(2,1)}, bf16[1024,1536]{1,0:T(8,128)(2,1)}, f32[12,1536]{1,0:T(8,128)}) custom-call(bf16[32,1536]{1,0:T(8,128)(2,1)} %bitcast.10, bf16[32,1536]{1,0:T(8,128)(2,1)} %bitcast.11, bf16[32,1536]{1,0:T(8,128)(2,1)} %bitcast.12, bf16[32,1536]{1,0:T(8,128)(2,1)} %bitcast.13, bf16[96,1536]{1,0:T(8,128)(2,1)} %bitcast.8, ...), custom_call_target="tpu_custom_call" | custom-call | flops 10499999744 | bytes 25000000 | tf_op jit(solution)/shard_map/pallas_call | solution.py:445
  72.8 1.5 %copy.22 = bf16[1,32,1536]{2,1,0:T(8,128)(2,1)} copy(bf16[1,32,1536]{2,1,0:T(8,128)(2,1)} %bitcast.7) | data formatting | bytes 196608
  74.4 0.0 copy-start
  74.4 3.8 %copy.23 = bf16[1024,1536]{1,0:T(8,128)(2,1)} copy(bf16[1024,1536]{1,0:T(8,128)(2,1)} %get-tuple-element.13) | data formatting | bytes 6291456
  78.2 0.0 copy-done
  78.2 0.6 copy.24
Async XLA Ops:
  74.4 3.8 %copy-start = (f32[12,1536]{1,0:T(8,128)S(1)}, f32[12,1536]{1,0:T(8,128)}, u32[]{:S(2)}) copy-start(f32[12,1536]{1,0:T(8,128)} %get-tuple-element.14) | copy-start | bytes 221188

commit v3 on v2

v3 whole, which is shorter than its diff:
```python
import functools

import jax
import jax.numpy as jnp
from jax import lax
from jax.experimental import pallas as pl
from jax.experimental.pallas import tpu as pltpu
from jax.sharding import PartitionSpec as P

HEADS = 12
HEAD = 128
FRAMES_GROUP = 3
WINDOW_FRAMES = 9
D = 1536
HALF = 768
BF = jnp.bfloat16
F32 = jnp.float32
MESH = pl.DeviceIdType.MESH


def rem(a, n):
    return lax.rem(a, jnp.int32(n))


def div(a, n):
    return lax.div(a, jnp.int32(n))


SCOPE = [None]


def sc(name=None):
    if SCOPE[0] is not None:
        SCOPE[0].__exit__(None, None, None)
    SCOPE[0] = None
    if name and PROFILE:
        SCOPE[0] = jax.named_scope(name)
        SCOPE[0].__enter__()


PROFILE = False
PRE = 2
MSG0 = (0, 2, 1)
MSG1 = ()


def owner(h):
    u, r = h // 3, h % 3
    zl = u // 2
    y = (u % 2) * 2 + (zl if r < 2 else 1 - zl)
    return zl * 8 + y * 2 + (r if r < 2 else 1)


def fused_kernel(
    stream_hbm, q_hbm, nk_hbm, nv_hbm, ck_hbm, cv_hbm, frames_hbm, group_hbm, step_hbm, gate_hbm, aow_hbm,
    cin_hbm, cot_hbm, w_hbm, so_ref, gin_hbm, gw_ref,
    stream_ref, frames_ref, group_ref, step_ref, gate_ref, w_ref,
    kbuf, vbuf, qbuf, aow, msg, got, ob, mixed,
    cin, cot, wown, tmp, wm, at, acc, dsend, drecv, rsend, rsend2,
    ra0, ra1, ra2, b0, b1, b2, b0s, b1s, b2s, rb0, rb1, rb2, fsend, frecv, obuf, gacc,
    ld_sem, p0_s, p0_r, g1_s, g1_r, g2_s, g2_r, push_s, push_r,
    d_s, d_r, a_s, a_r, b_s, b_r, f_s, f_r, o_sem, m_s, m_r, o_s, o_r,
):
    dp = lax.axis_index("dp")
    seq = lax.axis_index("seq")
    zh, x = div(dp, 4), rem(dp, 4)
    zl, y, c = div(seq, 8), div(rem(seq, 8), 2), rem(seq, 2)
    z = zh * 2 + zl
    xh, xl = div(x, 2), rem(x, 2)
    plane = y * 2 + c
    partner = (dp, seq + 1 - 2 * c)

    def xdev(xx):
        return (zh * 4 + xx, seq)

    def zdev(zz):
        return (div(zz, 2) * 4 + x, rem(zz, 2) * 8 + plane)

    def ydev(yy, cc):
        return (dp, zl * 8 + yy * 2 + cc)

    def rcopy(src, dst, s_sem, r_sem, dev):
        return pltpu.make_async_remote_copy(
            src_ref=src, dst_ref=dst, send_sem=s_sem, recv_sem=r_sem, device_id=dev, device_id_type=MESH
        )

    xs = [rem(x + s, 4) for s in (1, 2, 3)]
    ys = [rem(y + s, 4) for s in (1, 2, 3)]
    zs = [rem(z + s, 4) for s in (1, 2, 3)]
    plane_peers = [(rem(y + s, 4), c if k == 0 else 1 - c) for s in range(4) for k in range(2) if (s, k) != (0, 0)]
    others = [rem(seq + s, 16) for s in range(1, 16)]
    flat = [(rem(x + a, 4), rem(z + b, 4)) for a in range(4) for b in range(4) if (a, b) != (0, 0)]

    def xzdev(xx, zz):
        return (div(zz, 2) * 4 + xx, rem(zz, 2) * 8 + plane)


    sc("barrier")
    barrier = pltpu.get_barrier_semaphore()
    peers = [xdev(v) for v in xs] + [((1 - zh) * 4 + x, v * 8 + plane) for v in range(2)] + [(dp, v) for v in others]
    peers += [xzdev(a, b) for k, (a, b) in enumerate(flat) if (k + 1) // 4 and (k + 1) % 4]
    for dev in peers:
        pl.semaphore_signal(barrier, inc=1, device_id=dev, device_id_type=MESH)
    pairs = [(w_hbm, w_ref)]
    pairs += [(cot_hbm.at[:, pl.ds(h * HALF, HALF)], cot.at[h]) for h in range(2)]
    pairs += [(cin_hbm.at[:, pl.ds(t * 384, 384)], cin.at[t]) for t in range(4)]
    pairs += [(q_hbm, qbuf), (ck_hbm, kbuf.at[pl.ds(0, 96)]), (nk_hbm, kbuf.at[pl.ds(96, 32)]),
              (cv_hbm, vbuf.at[pl.ds(0, 96)]), (nv_hbm, vbuf.at[pl.ds(96, 32)]), (frames_hbm, frames_ref), (group_hbm, group_ref)]
    pairs += [(aow_hbm, aow), (stream_hbm, stream_ref), (gate_hbm, gate_ref), (step_hbm, step_ref)]
    loads = [pltpu.make_async_copy(a, b, ld_sem.at[k]) for k, (a, b) in enumerate(pairs)]
    for ld in loads:
        ld.start()

    p0 = [
        rcopy(wown.at[b], tmp.at[plane], p0_s.at[k], p0_r.at[k], ydev(a, b))
        for k, (a, b) in enumerate(plane_peers)
    ]

    def messages():
        for ld in loads[7:14]:
            ld.wait()
        first = FRAMES_GROUP * group_ref[0]
        frames = frames_ref[...]
        live = jnp.where((frames < first) & (frames >= first - WINDOW_FRAMES), 1.0, 0.0)
        live = jnp.broadcast_to(live, (16, 96)).astype(BF)
        for h in range(HEADS):
            cols = pl.ds(h * HEAD, HEAD)
            msg[h, pl.ds(0, 128), :] = kbuf[:, cols]
            msg[h, pl.ds(128, 128), :] = vbuf[:, cols]
            msg[h, pl.ds(256, 32), :] = qbuf[:, cols]
            msg[h, pl.ds(288, 16), :] = jnp.ones((16, HEAD), BF)
            msg[h, pl.ds(288, 16), pl.ds(0, 96)] = live

    def mcopy(h):
        return rcopy(msg.at[h], got.at[seq], m_s.at[h], m_r.at[seq], (dp, owner(h)))

    def send_messages(stage):
        for h in range(HEADS):
            same_z, same_y = zl == owner(h) // 8, y == owner(h) // 2 % 4
            if stage == 0:
                now = same_y & (seq != owner(h))
            elif stage == 1:
                now = same_z & jnp.logical_not(same_y)
            else:
                now = jnp.logical_not(same_z | same_y)

            @pl.when(now)
            def _():
                mcopy(h).start()

            if stage == 0:

                @pl.when(seq == owner(h))
                def _():
                    got[seq] = msg[h]

    def part2(ref, yy):
        return ref.at[..., pl.ds(pl.multiple_of(div(yy, 2) * 48, 48), 48), pl.ds(pl.multiple_of(512 + rem(yy, 2) * 128, 128), 128)]

    own = wm.at[c, zh, xh, xl, zl]
    g1 = []
    for k in range(3):
        g1.append(rcopy(own.at[:, pl.ds(0, 256)], own.at[:, pl.ds(0, 256)], g1_s.at[k], g1_r.at[k], xdev(xs[k])))
        g1.append(rcopy(own.at[:, pl.ds(256, 256)], own.at[:, pl.ds(256, 256)], g1_s.at[3 + k], g1_r.at[3 + k], zdev(zs[k])))
    for k, (a, b) in enumerate(flat):
        g1.append(rcopy(part2(own, y), part2(own, y), g1_s.at[6 + k], g1_r.at[6 + k], xzdev(a, b)))
    g2 = []
    w0 = wm.at[c, zh, :, :, zl, :, pl.ds(0, 256)]
    w1 = wm.at[c, :, xh, xl, :, :, pl.ds(256, 256)]
    w2 = part2(wm.at[c], y)
    for k in range(3):
        g2.append(rcopy(w0, w0, g2_s.at[k], g2_r.at[k], zdev(zs[k])))
        g2.append(rcopy(w1, w1, g2_s.at[3 + k], g2_r.at[3 + k], xdev(xs[k])))
        g2.append(rcopy(w2, w2, g2_s.at[6 + k], g2_r.at[6 + k], ydev(ys[k], c)))

    sc("ldwait")
    loads[0].wait()
    for h in range(2):
        wown[h] = jnp.zeros((16, HALF), BF)
        wown[h, pl.ds(0, 12), :] = w_ref[:, pl.ds(h * HALF, HALF)]
    for ld in loads[1:3]:
        ld.wait()
    sc()

    def dcopy(t):
        return rcopy(dsend.at[t], drecv.at[t], d_s.at[t], d_r.at[t], partner)

    def gw_tile(t):
        pltpu.make_async_copy(
            cin_hbm.at[:, pl.ds(pl.multiple_of(t * 384, 384), 384)], cin.at[t], ld_sem.at[3 + t]
        ).wait()
        at[...] = cin[t].T
        dsend[t] = lax.dot_general(
            at[...], cot[1 - c], (((1,), (0,)), ((), ())), preferred_element_type=F32
        ).astype(BF)
        acc[div(t, 2), rem(t, 2)] = lax.dot_general(
            at[...], cot[c], (((1,), (0,)), ((), ())), preferred_element_type=F32
        ).reshape(2, 2, 96, HALF)

    sc("gw0")

    @pl.loop(0, PRE)
    def _(t):
        gw_tile(t)

    sc("msg")
    messages()
    sc("barwait")
    pl.semaphore_wait(barrier, len(peers))
    for cp in p0:
        cp.start()
    tmp[plane] = wown[c]
    for t in range(PRE):
        dcopy(jnp.int32(t)).start()
    for k in MSG0:
        send_messages(k)
    sc("gw1")

    @pl.loop(PRE, 4)
    def _(t):
        gw_tile(t)
        dcopy(t).start()

    sc()

    sc("p0wait")
    for cp in p0:
        cp.wait_recv()
    row = lax.broadcasted_iota(jnp.int32, (96, 128), 0)
    col = lax.broadcasted_iota(jnp.int32, (96, 128), 1)
    pick = (col == div(row, 12) * 16 + rem(row, 12)).astype(BF)
    block = jnp.dot(pick, tmp[...].reshape(128, HALF), preferred_element_type=F32).astype(BF)
    own[:, pl.ds(0, 512)] = block[:, :512]
    for yy in range(4):
        i, j = yy // 2 * 48, 512 + yy % 2 * 128

        @pl.when(y == yy)
        def _():
            own[pl.ds(i, 48), pl.ds(j, 128)] = block[i : i + 48, j : j + 128]

    for cp in g1:
        cp.start()
    sc()

    @pl.loop(0, 4)
    def _(t):
        sc("dwait")
        dcopy(t).wait_recv()
        sc("chipsum")
        i, j = div(t, 2), rem(t, 2)
        both = acc[i, j] + drecv[t].reshape(2, 2, 96, HALF).astype(F32)
        acc[i, j] = both
        rsend[i, j] = both[..., :512].astype(BF)
        for yy in range(4):
            rsend2[yy, i, j] = both[:, :, (yy // 2) * 48 : (yy // 2) * 48 + 48, 512 + (yy % 2) * 128 : 640 + (yy % 2) * 128].astype(BF)
        sc()

    sc("rastart")
    ra = []
    for k in range(3):
        ra.append(rcopy(rsend.at[div(zs[k], 2), :, :, rem(zs[k], 2), :, pl.ds(0, 256)], ra0.at[k], a_s.at[k], a_r.at[k], zdev(zs[k])))
        ra.append(rcopy(rsend.at[:, div(xs[k], 2), rem(xs[k], 2), :, :, pl.ds(256, 256)], ra1.at[k], a_s.at[3 + k], a_r.at[3 + k], xdev(xs[k])))
        ra.append(rcopy(rsend2.at[ys[k]], ra2.at[k], a_s.at[6 + k], a_r.at[6 + k], ydev(ys[k], c)))
    for cp in ra:
        cp.start()
    for k in MSG1:
        send_messages(k)

    sc("g1wait")
    for cp in g1:
        cp.wait_recv()
    for cp in g2:
        cp.start()

    double = rem(y, 2) == zl
    active = double | (c == 1)
    head = 3 * (zl * 2 + div(y, 2)) + jnp.where(double, c, 2)

    def mixcopy(k):
        return rcopy(ob.at[others[k]], mixed.at[head], o_s.at[k], o_r.at[head], (dp, others[k]))

    sc("attwait")

    @pl.when(active)
    def _():
        for src in others:
            rcopy(msg.at[0], got.at[src], m_s.at[0], m_r.at[src], partner).wait_recv()

    sc("att")

    @pl.when(active)
    def _():
        alive = jnp.concatenate([got[j, pl.ds(288, 16), :] for j in range(16)], axis=1)[0:1].astype(F32) > 0.5

        @pl.loop(0, 4)
        def _(i):
            q = got[pl.ds(i * 4, 4), pl.ds(256, 32), :].reshape(128, HEAD)
            keys = got[:, pl.ds(0, 128), :].reshape(2048, HEAD)
            values = got[:, pl.ds(128, 128), :].reshape(2048, HEAD)
            scores = lax.dot_general(q, keys, (((1,), (1,)), ((), ())), preferred_element_type=F32) * (HEAD ** (-0.5))
            scores = jnp.where(alive, scores, -1e30)
            top = jnp.max(scores, axis=1, keepdims=True)
            weights = jnp.where(alive, jnp.exp(scores - top), 0.0)
            totals = jnp.sum(weights, axis=1, keepdims=True)
            summed = jnp.dot(weights.astype(BF), values, preferred_element_type=F32)
            ob[pl.ds(i * 4, 4)] = (summed / totals).astype(BF).reshape(4, 32, HEAD)

        for k in range(15):
            mixcopy(k).start()
        mixed[head] = ob[seq]

    sc("rawait")
    for cp in ra:
        cp.wait_recv()
    v0 = acc[zh, :, :, zl, :, 0:256]
    v1 = acc[:, xh, xl, :, :, 256:512]
    for k in range(3):
        v0 = v0 + ra0[k].astype(F32)
        v1 = v1 + ra1[k].astype(F32)
    b0[...] = v0
    b1[...] = v1
    b0s[...] = v0.astype(BF)
    b1s[...] = v1.astype(BF)
    v2 = rsend2[y].astype(F32)
    for k in range(3):
        v2 = v2 + ra2[k].astype(F32)
    b2[...] = v2
    b2s[...] = v2.astype(BF)
    rb = []
    for k in range(3):
        rb.append(rcopy(b0s.at[div(xs[k], 2), rem(xs[k], 2)], rb0.at[k], b_s.at[k], b_r.at[k], xdev(xs[k])))
        rb.append(rcopy(b1s.at[div(zs[k], 2), rem(zs[k], 2)], rb1.at[k], b_s.at[3 + k], b_r.at[3 + k], zdev(zs[k])))
    for k, (a, b) in enumerate(flat):
        src = b2s.at[div(b, 2), div(a, 2), rem(a, 2), rem(b, 2)]
        rb.append(rcopy(src, rb2.at[k], b_s.at[6 + k], b_r.at[6 + k], xzdev(a, b)))

    for cp in rb:
        cp.start()
    def pcopy(k, t):
        src = wm.at[c, div(t, 2), rem(t, 2), :, :, :, pl.ds(256 - 256 * k, 512 - 256 * k)]
        return rcopy(src, src, push_s.at[4 * k + t], push_r.at[4 * k + t], partner)

    sc("g2wait")
    for cp in g2[1::3] + g2[2::3]:
        cp.wait_recv()
    for t in range(4):
        pcopy(0, jnp.int32(t)).start()
    sc()

    def ocopy(t):
        return pltpu.make_async_copy(obuf.at[t], gin_hbm.at[:, pl.ds(pl.multiple_of(t * 384, 384), 384)], o_sem.at[t])

    def gin_part(t, lo, width):
        i, j = div(t, 2), rem(t, 2)
        dims = (((1,), (1,)), ((), ()))
        cols = pl.ds(lo, width)
        res = lax.dot_general(cot[0, :, cols], wm[0, i, j, :, :, :, cols].reshape(384, width), dims, preferred_element_type=F32)
        return res + lax.dot_general(cot[1, :, cols], wm[1, i, j, :, :, :, cols].reshape(384, width), dims, preferred_element_type=F32)

    @pl.loop(0, 4)
    def _(t):
        sc("pwait")
        pcopy(0, t).wait_recv()
        sc("gin")
        gacc[t] = gin_part(t, 256, 512)
        sc()

    sc("rbwait2")
    for cp in rb:
        cp.wait_recv()
    r0 = b0[xh, xl]
    r1 = b1[zh, zl]
    for k in range(3):
        r0 = r0 + rb0[k].astype(F32)
        r1 = r1 + rb1[k].astype(F32)
    sc("last")
    r2 = b2[zh, xh, xl, zl]
    for k in range(15):
        r2 = r2 + rb2[k].astype(F32)

    row = lax.broadcasted_iota(jnp.int32, (96, 256), 0)
    col = lax.broadcasted_iota(jnp.int32, (96, 256), 1)
    mine = (div(row, 48) == div(y, 2)) & (div(col, 128) == rem(y, 2))
    r2 = jnp.concatenate([r2, r2], axis=0)
    r2 = jnp.where(mine, jnp.concatenate([r2, r2], axis=1), 0.0)
    row = lax.broadcasted_iota(jnp.int32, (128, 96), 0)
    col = lax.broadcasted_iota(jnp.int32, (128, 96), 1)
    place = ((col == div(row, 16) * 12 + rem(row, 16)) & (rem(row, 16) < 12)).astype(BF)
    full = jnp.concatenate([r0, r1, r2], axis=1).astype(BF)
    fsend[...] = jnp.dot(place, full, preferred_element_type=F32).astype(BF).reshape(8, 16, HALF)
    fin = [
        rcopy(fsend.at[a * 2 + b], frecv.at[plane], f_s.at[k], f_r.at[k], ydev(a, b))
        for k, (a, b) in enumerate(plane_peers)
    ]
    for cp in fin:
        cp.start()
    frecv[plane] = fsend[plane]

    sc("g2wait2")
    for cp in g2[0::3]:
        cp.wait_recv()
    for t in range(4):
        pcopy(1, jnp.int32(t)).start()

    sc("mixwait")
    for h in range(HEADS):

        @pl.when(seq != owner(h))
        def _():
            rcopy(ob.at[0], mixed.at[h], o_s.at[0], o_r.at[h], partner).wait_recv()

    for ld in loads[14:]:
        ld.wait()
    sc("proj")
    joined = jnp.concatenate([mixed[h] for h in range(HEADS)], axis=1)
    projected = jnp.dot(joined, aow[...], preferred_element_type=F32)
    row = lax.broadcasted_iota(jnp.int32, (4, D), 0)
    gate = jnp.sum(jnp.where(row == step_ref[0], gate_ref[...], 0.0), axis=0, keepdims=True)
    so_ref[...] = (stream_ref[...].astype(F32) + gate * projected).astype(BF)

    sc()

    @pl.loop(0, 4)
    def _(t):
        sc("pwait")
        pcopy(1, t).wait_recv()
        sc("gin")
        obuf[t] = (gacc[t] + gin_part(t, 0, 256)).astype(BF)
        ocopy(t).start()
        sc()

    sc("finwait")
    for cp in fin:
        cp.wait_recv()
    sc("drain")
    factor = float(131072) ** (-0.5)
    for h in range(2):
        total = frecv[h].astype(F32)
        for yy in range(1, 4):
            total = total + frecv[yy * 2 + h].astype(F32)
        gw_ref[:, pl.ds(h * HALF, HALF)] = total[:12] * factor

    for cp in p0 + g1 + g2 + ra + rb + fin:
        cp.wait_send()
    for t in range(4):
        dcopy(jnp.int32(t)).wait_send()
        pcopy(0, jnp.int32(t)).wait_send()
        pcopy(1, jnp.int32(t)).wait_send()
        ocopy(jnp.int32(t)).wait()
    for h in range(HEADS):

        @pl.when(seq != owner(h))
        def _():
            mcopy(h).wait_send()

    @pl.when(active)
    def _():
        for k in range(15):
            mixcopy(k).wait_send()

    sc()


def local(stream, queries, new_keys, new_values, cache_keys, cache_values, cache_frames, group_index, timestep, gate_table, attn_out_weight, critic_in, critic_cot, critic_weight):
    dma = pltpu.SemaphoreType.DMA
    V = pltpu.VMEM
    anywhere = pl.BlockSpec(memory_space=pl.ANY)
    vmem = pl.BlockSpec(memory_space=pltpu.VMEM)
    so, gin, gw = pl.pallas_call(
        fused_kernel,
        out_shape=(
            jax.ShapeDtypeStruct((32, D), BF),
            jax.ShapeDtypeStruct((1024, D), BF),
            jax.ShapeDtypeStruct((12, D), F32),
        ),
        in_specs=[anywhere] * 14,
        out_specs=(vmem, anywhere, vmem),
        scratch_shapes=[
            V((32, D), BF), V((1, 96), jnp.int32), pltpu.SMEM((1,), jnp.int32), pltpu.SMEM((1,), jnp.int32), V((4, D), F32), V((12, D), BF),
            V((128, D), BF), V((128, D), BF), V((32, D), BF), V((D, D), BF), V((HEADS, 304, HEAD), BF),
            V((16, 304, HEAD), BF), V((16, 32, HEAD), BF), V((HEADS, 32, HEAD), BF),
            V((4, 1024, 384), BF), V((2, 1024, HALF), BF), V((2, 16, HALF), BF), V((8, 16, HALF), BF),
            V((2, 2, 2, 2, 2, 96, HALF), BF), V((384, 1024), BF), V((2, 2, 2, 2, 96, HALF), F32),
            V((4, 384, HALF), BF), V((4, 384, HALF), BF),
            V((2, 2, 2, 2, 96, 512), BF), V((4, 2, 2, 2, 2, 48, 128), BF),
            V((3, 2, 2, 96, 256), BF), V((3, 2, 2, 96, 256), BF), V((3, 2, 2, 2, 2, 48, 128), BF),
            V((2, 2, 96, 256), F32), V((2, 2, 96, 256), F32), V((2, 2, 2, 2, 48, 128), F32),
            V((2, 2, 96, 256), BF), V((2, 2, 96, 256), BF), V((2, 2, 2, 2, 48, 128), BF),
            V((3, 96, 256), BF), V((3, 96, 256), BF), V((15, 48, 128), BF),
            V((8, 16, HALF), BF), V((8, 16, HALF), BF), V((4, 1024, 384), BF), V((4, 1024, 384), F32),
            dma((18,)), dma((7,)), dma((7,)), dma((21,)), dma((21,)), dma((9,)), dma((9,)),
            dma((8,)), dma((8,)), dma((4,)), dma((4,)), dma((9,)), dma((9,)), dma((21,)), dma((21,)),
            dma((7,)), dma((7,)), dma((4,)), dma((12,)), dma((16,)), dma((15,)), dma((12,)),
        ],
        compiler_params=pltpu.CompilerParams(
            collective_id=0, has_side_effects=True, vmem_limit_bytes=60 * 1024 * 1024
        ),
        cost_estimate=pl.CostEstimate(flops=10500000000, bytes_accessed=25000000, transcendentals=1000000),
    )(
        stream[0], queries[0], new_keys[0], new_values[0], cache_keys[0], cache_values[0], cache_frames,
        group_index, timestep, gate_table, attn_out_weight, critic_in, critic_cot, critic_weight,
    )
    return (so[None], gin, gw)


def solution(mesh):
    three = P("dp", "seq", None)
    rows = P(("dp", "seq"), None)
    return jax.shard_map(
        local,
        mesh=mesh,
        in_specs=(three,) * 6 + (P("dp", "seq"), P("dp"), P("dp"), P(), P(), rows, rows, rows),
        out_specs=(three, rows, rows),
        check_vma=False,
    )
```

time: 79 us -> 67.5 us (0.85)
  Pallas kernels: 70.9 us -> 59.4 us
    pallas_call x1, Pallas kernels: 70.9 us -> 59.4 us  [local(): pl.pallas_call(fused_kernel, out_shape=(jax.ShapeDtypeStruct((32, D), BF)...]
where the time goes in v3:
time: 67.5 us; the launch traced here: 67.3 us
  Pallas kernels  59.4 us (88%)
  local copies, waits for them, and re-layouts  5.97 us (9%)
  between operations  1.94 us (3%)
    pallas_call x1, Pallas kernels, local(): pl.pallas_call(fused_kernel, out_shape=(jax.ShapeDtypeStruct((32, D), BF)...  59.4 us
    unnamed x5, local copies, waits for them, and re-layouts  5.97 us

profile of v3, /device:TPU:1, one launch (start us, length us, event | category | flops | bytes accessed | tf_op | source)
XLA Modules:
  0.0 67.3 jit_solution(13834025326306536867)
XLA Ops:
  1.9 59.4 %shard_map.157 = (bf16[32,1536]{1,0:T(8,128)(2,1)}, bf16[1024,1536]{1,0:T(8,128)(2,1)}, f32[12,1536]{1,0:T(8,128)}) custom-call(bf16[32,1536]{1,0:T(8,128)(2,1)} %bitcast.10, bf16[32,1536]{1,0:T(8,128)(2,1)} %bitcast.11, bf16[32,1536]{1,0:T(8,128)(2,1)} %bitcast.12, bf16[32,1536]{1,0:T(8,128)(2,1)} %bitcast.13, bf16[96,1536]{1,0:T(8,128)(2,1)} %bitcast.8, ...), custom_call_target="tpu_custom_call" | custom-call | flops 10499999744 | bytes 25000000 | tf_op jit(solution)/shard_map/pallas_call | solution.py:469
  61.4 1.5 %copy.22 = bf16[1,32,1536]{2,1,0:T(8,128)(2,1)} copy(bf16[1,32,1536]{2,1,0:T(8,128)(2,1)} %bitcast.7) | data formatting | bytes 196608
  62.9 0.0 copy-start
  62.9 3.8 %copy.23 = bf16[1024,1536]{1,0:T(8,128)(2,1)} copy(bf16[1024,1536]{1,0:T(8,128)(2,1)} %get-tuple-element.13) | data formatting | bytes 6291456
  66.7 0.0 copy-done
  66.7 0.6 copy.24
Async XLA Ops:
  62.9 3.8 %copy-start = (f32[12,1536]{1,0:T(8,128)S(1)}, f32[12,1536]{1,0:T(8,128)}, u32[]{:S(2)}) copy-start(f32[12,1536]{1,0:T(8,128)} %get-tuple-element.14) | copy-start | bytes 221188
